TPU v7x, 32 devices: a whole 2x2x4 slice. The times are simulated.
32 devices in a mesh: dp: 8 (over z, x), mp: 4 (over y, core).
Axes of the slice: x: 2, y: 2, z: 4, core: 2. Of those that a mesh axis runs over, the one named last changes fastest.
Arguments:
- partials: bfloat16 [8, 256, 8192], P('dp', None, 'mp'), may hold values from -11 to 11
- momentum: float32 [32, 256, 256], P(('dp', 'mp')), may hold values from -0.3 to 0.3
- second: float32 [32, 256, 256], P(('dp', 'mp')), may hold values from 0.0002 to 0.02
- left_stat: float32 [32, 256, 256], P(('dp', 'mp')), may hold values from -36 to 36.5, as said below
- right_stat: float32 [32, 256, 256], P(('dp', 'mp')), may hold values from -36 to 36.5, as said below
- left_basis: float32 [32, 256, 256], P(('dp', 'mp')), may hold values from -1 to 1, as said below
- right_basis: float32 [32, 256, 256], P(('dp', 'mp')), may hold values from -1 to 1, as said below
Outputs:
- update: bfloat16 [256, 8192], P(None, 'mp')
- momentum_new: float32 [32, 256, 256], P(('dp', 'mp'))
- second_new: float32 [32, 256, 256], P(('dp', 'mp'))
- left_new: float32 [32, 256, 256], P(('dp', 'mp'))
- right_new: float32 [32, 256, 256], P(('dp', 'mp'))
- left_basis_new: float32 [32, 256, 256], P(('dp', 'mp'))
- right_basis_new: float32 [32, 256, 256], P(('dp', 'mp'))
Inputs may be any that keep to these rules, and one draw needn't show every extreme that they name: `left_stat`: each block is symmetric positive definite. `right_stat`: each block is symmetric positive definite. `left_basis`: each block is an orthogonal matrix. `right_basis`: each block is an orthogonal matrix.
All inputs are finite; a program needn't handle non-finite values.
Results may differ from a plain program's by a relative error of at most 0.00045.
Values may be sent and summed in bfloat16 or wider, within the bound.
No kernel may reach another device: no remote copies, remote signals or barrier semaphores. Data moves between devices by JAX's collectives and lax.ppermute only.
A program may use at most 128 MiB of HBM per device.

v0:
```python
import jax
import jax.numpy as jnp
from jax import lax
from jax.sharding import PartitionSpec as P

beta_first = 0.9
beta_second = 0.95
epsilon = 1e-08
highest = lax.Precision.HIGHEST


def product(left, right):
    return jnp.einsum("tij,tjk->tik", left, right, precision=highest)


def inner_left(left, right):
    return jnp.einsum("tji,tjk->tik", left, right, precision=highest)


def outer_right(left, right):
    return jnp.einsum("tij,tkj->tik", left, right, precision=highest)


def refresh(statistic, basis):
    powered = product(statistic, basis)
    factor = jnp.linalg.cholesky(inner_left(powered, powered))
    return lax.linalg.triangular_solve(
        factor, powered, left_side=False, lower=True, transpose_a=True
    )


def on_device(partials, momentum, second, left_stat, right_stat, left_basis, right_basis):
    block_size = left_basis.shape[1]
    replica_part = partials[0]
    row_count, shard_width = replica_part.shape
    row_bands = row_count // block_size
    col_bands = shard_width // block_size
    stacked = replica_part.reshape(row_bands, block_size, col_bands, block_size)
    stacked = jnp.transpose(stacked, (0, 2, 1, 3)).reshape(
        row_bands * col_bands, block_size, block_size
    )
    gradient = lax.psum_scatter(stacked.astype(jnp.float32), "dp", scatter_dimension=0, tiled=True)
    grad_local = jnp.sum(gradient * gradient)
    grad_norm = lax.psum(grad_local, ("dp", "mp"))
    left_new = beta_second * left_stat + (1.0 - beta_second) * outer_right(gradient, gradient)
    right_new = beta_second * right_stat + (1.0 - beta_second) * inner_left(gradient, gradient)
    momentum_new = beta_first * momentum + (1.0 - beta_first) * gradient
    grad_rot = product(inner_left(left_basis, gradient), right_basis)
    moment_rot = product(inner_left(left_basis, momentum_new), right_basis)
    second_new = beta_second * second + (1.0 - beta_second) * grad_rot * grad_rot
    direction = moment_rot / (jnp.sqrt(second_new) + epsilon)
    step_local = jnp.sum(direction * direction)
    step_norm = lax.psum(step_local, ("dp", "mp"))
    raw_step = outer_right(product(left_basis, direction), right_basis)
    update = (raw_step * jnp.sqrt(grad_norm / step_norm)).astype(jnp.bfloat16)
    gathered = lax.all_gather(update, "dp", axis=0, tiled=True)
    assembled = gathered.reshape(row_bands, col_bands, block_size, block_size)
    assembled = jnp.transpose(assembled, (0, 2, 1, 3)).reshape(row_count, shard_width)
    left_basis_new = refresh(left_new, left_basis)
    right_basis_new = refresh(right_new, right_basis)
    return (
        assembled,
        momentum_new,
        second_new,
        left_new,
        right_new,
        left_basis_new,
        right_basis_new,
    )


def solution(mesh):
    in_specs = (
        P("dp", None, "mp"),
        P(("dp", "mp"), None, None),
        P(("dp", "mp"), None, None),
        P(("dp", "mp"), None, None),
        P(("dp", "mp"), None, None),
        P(("dp", "mp"), None, None),
        P(("dp", "mp"), None, None),
    )
    out_specs = (
        P(None, "mp"),
        P(("dp", "mp"), None, None),
        P(("dp", "mp"), None, None),
        P(("dp", "mp"), None, None),
        P(("dp", "mp"), None, None),
        P(("dp", "mp"), None, None),
        P(("dp", "mp"), None, None),
    )
    return jax.shard_map(
        on_device, mesh=mesh, in_specs=in_specs, out_specs=out_specs, check_vma=False
    )
```

profile of v0, /device:TPU:0, one launch (start us, length us, event | category | flops | bytes accessed | tf_op | source)
XLA Modules:
  0.0 267.8 jit_solution(7324107700456194609)
XLA Ops:
  7.2 0.0 copy-start
  7.2 0.0 reduce-scatter.2.cloned.1.call-start
  7.2 1.5 copy.22
  8.7 0.0 copy-start.7
  8.8 1.5 convert_bitcast_fusion
  10.3 0.0 reduce-scatter.2.cloned.1.call-update
  10.3 0.0 all-gather.3.cloned.1.call-start
  10.4 0.1 copy.21
  10.5 72.8 %reduce-scatter.2.cloned.1.call-done = f32[1,256,256]{1,2,0:T(8,128)} async-done(((f32[8,256,256]{1,2,0:T(8,128)}), f32[1,256,256]{1,2,0:T(8,128)}) %reduce-scatter.2.cloned.1.call-update) | async-done | bytes 262160 | tf_op jit(solution)/shard_map/reduce_scatter | solution.py:42
  83.3 1.7 multiply_reduce_fusion.1
  85.0 0.8 copy.28
  85.8 0.4 fusion.36
  86.2 0.6 fusion.24
  86.9 0.4 fusion.13
  87.3 0.0 copy-start.9
  87.3 1.2 multiply_reduce_fusion
  88.5 0.6 fusion.20
  89.1 39.9 %all-reduce.1 = (f32[]{:T(128)}, f32[]{:T(128)}) all-reduce(f32[]{:T(128)} %get-tuple-element.61, f32[]{:T(128)} %get-tuple-element.71), channel_id=1, replica_groups=mesh['dp'=8,'mp'=4] {'dp','mp'}, use_global_device_ids=true, to_apply=%region_2.0 | all-reduce | flops 2 | bytes 16 | tf_op jit(solution)/shard_map/psum | solution.py:44
  130.4 1.3 fusion.4
  131.6 0.0 all-gather.3.cloned.1.call-update
  131.7 0.6 fusion.2
  132.3 0.0 copy-start.3
  132.3 0.4 fusion.18
  132.7 0.6 fusion.47
  133.3 0.1 copy.25
  133.5 11.7 %custom-call.17 = f32[1,128,128]{2,1,0:T(8,128)S(1)} custom-call(f32[1,128,128]{2,1,0:T(8,128)S(1)} %cholesky.191), custom_call_target="Cholesky" | custom-call | tf_op jit(solution)/shard_map/jit(cholesky)/cholesky | solution.py:26
  145.2 9.8 %custom-call.18 = f32[1,1,128,128]{2,3,1,0:T(8,128)S(1)} custom-call(f32[1,1,128,128]{3,2,1,0:T(8,128)S(1)} %get-tuple-element.70), custom_call_target="InvertDiagBlocksLowerTriangular" | custom-call | tf_op jit(solution)/shard_map/jit(cholesky)/cholesky | solution.py:26
  155.1 0.2 bitcast_dynamic-update-slice_fusion.3
  155.3 0.3 fusion.9
  155.5 11.9 %custom-call.19 = f32[1,128,128]{2,1,0:T(8,128)S(1)} custom-call(f32[1,128,128]{2,1,0:T(8,128)S(1)} %fusion.9), custom_call_target="Cholesky" | custom-call | tf_op jit(solution)/shard_map/jit(cholesky)/cholesky | solution.py:26
  167.4 0.6 compare_reduce_fusion.2
  169.4 0.1 broadcast.104
  169.5 4.0 %while.4 = (s32[]{:T(128)}, f32[1,256,256]{2,1,0:T(8,128)S(1)}, s32[2,2]{1,0:T(2,128)S(1)}, f32[2,1,128,128]{3,2,1,0:T(8,128)S(1)}, s32[]{:T(128)}) while((s32[]{:T(128)}, f32[1,256,256]{2,1,0:T(8,128)S(1)}, s32[2,2]{1,0:T(2,128)S(1)}, f32[2,1,128,128]{3,2,1,0:T(8,128)S(1)}, s32[]{:T(128)}) %tuple.52), condition=%wide.while_cond, body=%wide.while_body.sunk | while | flops 2 | bytes 131189 | solution.py:27
  169.5 0.6 fusion.66
  170.1 1.4 bitcast_dynamic-update-slice_fusion.6
  171.5 0.6 fusion.66
  172.1 1.4 bitcast_dynamic-update-slice_fusion.6
  173.5 19.7 %custom-call.20 = f32[1,2,128,128]{2,3,1,0:T(8,128)S(1)} custom-call(f32[1,2,128,128]{3,2,1,0:T(8,128)S(1)} %bitcast.220), custom_call_target="InvertDiagBlocksLowerTriangular" | custom-call | tf_op jit(solution)/shard_map/triangular_solve/custom-call.0 | solution.py:27
  193.2 0.3 fusion.40
  193.5 0.4 fusion.6
  193.9 0.3 convolution_bitcast_fusion.3
  194.3 0.8 copy.29
  195.1 0.4 fusion.3
  195.5 0.0 copy-start.4
  195.6 0.4 fusion.16
  195.9 0.6 fusion.48
  196.5 0.1 copy.27
  196.7 11.7 %custom-call.21 = f32[1,128,128]{2,1,0:T(8,128)S(1)} custom-call(f32[1,128,128]{2,1,0:T(8,128)S(1)} %cholesky.194), custom_call_target="Cholesky" | custom-call | tf_op jit(solution)/shard_map/jit(cholesky)/cholesky | solution.py:26
  208.5 9.8 %custom-call.22 = f32[1,1,128,128]{2,3,1,0:T(8,128)S(1)} custom-call(f32[1,1,128,128]{3,2,1,0:T(8,128)S(1)} %get-tuple-element.66), custom_call_target="InvertDiagBlocksLowerTriangular" | custom-call | tf_op jit(solution)/shard_map/jit(cholesky)/cholesky | solution.py:26
  218.3 0.2 bitcast_dynamic-update-slice_fusion.2
  218.5 0.3 fusion.10
  218.8 11.9 %custom-call.23 = f32[1,128,128]{2,1,0:T(8,128)S(1)} custom-call(f32[1,128,128]{2,1,0:T(8,128)S(1)} %fusion.10), custom_call_target="Cholesky" | custom-call | tf_op jit(solution)/shard_map/jit(cholesky)/cholesky | solution.py:26
  230.8 0.7 compare_reduce_fusion
  232.9 4.1 %while.5 = (s32[]{:T(128)}, f32[1,256,256]{2,1,0:T(8,128)S(1)}, s32[2,2]{1,0:T(2,128)S(1)}, f32[2,1,128,128]{3,2,1,0:T(8,128)S(1)}, s32[]{:T(128)}) while((s32[]{:T(128)}, f32[1,256,256]{2,1,0:T(8,128)S(1)}, s32[2,2]{1,0:T(2,128)S(1)}, f32[2,1,128,128]{3,2,1,0:T(8,128)S(1)}, s32[]{:T(128)}) %tuple.62), condition=%wide.while_cond.clone, body=%wide.while_body.clone.sunk | while | flops 2 | bytes 131189 | solution.py:27
  232.9 0.6 fusion.67
  233.5 1.4 bitcast_dynamic-update-slice_fusion.7
  235.0 0.6 fusion.67
  235.6 1.4 bitcast_dynamic-update-slice_fusion.7
  237.0 19.7 %custom-call.24 = f32[1,2,128,128]{2,3,1,0:T(8,128)S(1)} custom-call(f32[1,2,128,128]{3,2,1,0:T(8,128)S(1)} %bitcast.219), custom_call_target="InvertDiagBlocksLowerTriangular" | custom-call | tf_op jit(solution)/shard_map/triangular_solve/custom-call.0 | solution.py:27
  256.7 0.3 fusion.39
  257.0 0.4 fusion.8
  257.4 0.3 convolution_bitcast_fusion.1
  257.8 0.8 copy.30
  258.6 2.3 copy.33
  (37 shorter events, 0.5 us)
Async XLA Ops:
  7.2 79.7 %copy-start = (f32[1,256,256]{2,1,0:T(8,128)S(1)}, f32[1,256,256]{2,1,0:T(8,128)}, u32[]{:S(2)}) copy-start(f32[1,256,256]{2,1,0:T(8,128)} %param.16) | copy-start | bytes 786436
  7.2 76.1 %reduce-scatter.2.cloned.1.call-start = ((), (), s32[]{:S(2)}) async-start(), calls=%async_computation.1 | async-start | bytes 2359296 | tf_op jit(solution)/shard_map/reduce_scatter | solution.py:42
  8.7 1.6 copy-start.7
  10.3 75.5 %copy-start.1 = (f32[1,256,256]{2,1,0:T(8,128)S(1)}, f32[1,256,256]{2,1,0:T(8,128)}, u32[]{:S(2)}) copy-start(f32[1,256,256]{2,1,0:T(8,128)} %param.15) | copy-start | bytes 786436
  10.3 76.5 %copy-start.8 = (f32[1,256,256]{2,1,0:T(8,128)S(1)}, f32[1,256,256]{2,1,0:T(8,128)}, u32[]{:S(2)}) copy-start(f32[1,256,256]{2,1,0:T(8,128)} %param.12) | copy-start | bytes 786436
  10.3 248.2 %all-gather.3.cloned.1.call-start = ((), (), s32[]{:S(2)}) async-start(), calls=%async_computation.2 | async-start | bytes 1179648 | tf_op jit(solution)/shard_map/all_gather | solution.py:56
  83.3 2.9 %copy-start.2 = (f32[1,256,256]{1,2,0:T(8,128)S(1)}, f32[1,256,256]{1,2,0:T(8,128)}, u32[]{:S(2)}) copy-start(f32[1,256,256]{1,2,0:T(8,128)} %reduce-scatter.2.cloned.1.call-done) | copy-start | bytes 786436
  86.8 44.8 %copy-start.5 = (f32[1,256,256]{2,1,0:T(8,128)S(1)}, f32[1,256,256]{2,1,0:T(8,128)}, u32[]{:S(2)}) copy-start(f32[1,256,256]{2,1,0:T(8,128)} %param.13) | copy-start | bytes 786436
  87.3 45.4 %copy-start.9 = (f32[1,256,256]{2,1,0:T(8,128)}, f32[1,256,256]{2,1,0:T(8,128)S(1)}, u32[]{:S(2)}) copy-start(f32[1,256,256]{2,1,0:T(8,128)S(1)} %fusion.13) | copy-start | bytes 786436
  132.3 37.2 %copy-start.3 = (f32[1,256,256]{2,1,0:T(8,128)}, f32[1,256,256]{2,1,0:T(8,128)S(1)}, u32[]{:S(2)}) copy-start(f32[1,256,256]{2,1,0:T(8,128)S(1)} %fusion.2) | copy-start | bytes 786436
  155.3 39.9 %copy-start.6 = (f32[1,256,256]{2,1,0:T(8,128)S(1)}, f32[1,256,256]{2,1,0:T(8,128)}, u32[]{:S(2)}) copy-start(f32[1,256,256]{2,1,0:T(8,128)} %param.14) | copy-start | bytes 786436
  195.5 37.3 %copy-start.4 = (f32[1,256,256]{2,1,0:T(8,128)}, f32[1,256,256]{2,1,0:T(8,128)S(1)}, u32[]{:S(2)}) copy-start(f32[1,256,256]{2,1,0:T(8,128)S(1)} %fusion.3) | copy-start | bytes 786436
Sparse Core Ops, SparseCore 0:
  11.5 71.7 reduce-scatter.1
  131.8 40.2 all-gather.2
where the time goes:
time: 268 us
  other arithmetic  111 us (41%)
  waiting for transfers between devices  72.8 us (27%)
  blocking collectives  39.9 us (15%)
  between operations  18.5 us (7%)
  local copies, waits for them, and re-layouts  14.9 us (6%)
  matrix products  10.3 us (4%)
    reduce_scatter x1, waiting for transfers between devices, on_device(): lax.psum_scatter(stacked.astype(jnp.float32), 'dp', scatter_dimension=0,...  72.8 us
    another operation x12, other arithmetic, refresh(): factor = jnp.linalg.cholesky(inner_left(powered, powered))  68.3 us
    psum x1, blocking collectives, on_device(): grad_norm = lax.psum(grad_local, ('dp', 'mp'))  39.9 us
    another operation x7, other arithmetic, refresh(): lax.linalg.triangular_solve(factor, powered, left_side=False, lower=True,...  39.5 us
    another operation x15, local copies, waits for them, and re-layouts, refresh(): lax.linalg.triangular_solve(factor, powered, left_side=False, lower=True,...  8.1 us
    unnamed x26, local copies, waits for them, and re-layouts  6.54 us
  transfers between devices with their start and end apart: 2, of which 1 were waited for; matrix products, arithmetic and copies ran while one was open for 46% of the time, Pallas kernels for 0%

commit v1 on v0

v1 whole, which is shorter than its diff:
```python
import jax
import jax.numpy as jnp
from jax import lax
from jax.experimental import pallas as pl
from jax.experimental.pallas import tpu as pltpu
from jax.sharding import PartitionSpec as P

beta_first = 0.9
beta_second = 0.95
epsilon = 1e-08
highest = lax.Precision.HIGHEST
SUB = 8
LANES = 128
PANEL = 32


def product(left, right):
    return jnp.einsum("tij,tjk->tik", left, right, precision=highest)


def inner_left(left, right):
    return jnp.einsum("tji,tjk->tik", left, right, precision=highest)


def outer_right(left, right):
    return jnp.einsum("tij,tkj->tik", left, right, precision=highest)


def dot(left, right, left_dim, right_dim):
    return lax.dot_general(
        left,
        right,
        (((left_dim,), (right_dim,)), ((), ())),
        precision=highest,
        preferred_element_type=jnp.float32,
    )


def split(value):
    high = value.astype(jnp.bfloat16)
    rest = value - high.astype(jnp.float32)
    middle = rest.astype(jnp.bfloat16)
    low = (rest - middle.astype(jnp.float32)).astype(jnp.bfloat16)
    return high, middle, low


def lane(value, at):
    return jnp.broadcast_to(value[:, at:at + 1], (SUB, LANES))


def row(value, at):
    return jnp.broadcast_to(value[at:at + 1, :], (SUB, LANES))


def eliminate(work, order, rows):
    tiles = 2 * order // LANES
    groups = PANEL // SUB
    for start in range(0, order, PANEL):
        first = start // LANES
        live = range(first, tiles)
        held = [
            {v: work[start + SUB * h:start + SUB * (h + 1), v * LANES:(v + 1) * LANES] for v in live}
            for h in range(groups)
        ]
        for g in range(groups):
            at = (start + SUB * g) % LANES
            cols = {h: [lane(held[h][first], at + k) for k in range(SUB)] for h in range(g, groups)}
            yield
            for k in range(SUB):
                inverse = lax.rsqrt(row(cols[g][k], k))
                factor = {h: cols[h][k] * inverse for h in range(g, groups)}
                below = jnp.where(rows > k, factor[g], 0.0)
                for l in range(k + 1, SUB):
                    pivot = row(factor[g], l)
                    cols[g][l] = cols[g][l] - below * pivot
                    for h in range(g + 1, groups):
                        cols[h][l] = cols[h][l] - factor[h] * pivot
                for v in live:
                    top = row(held[g][v], k) * inverse
                    held[g][v] = jnp.where(rows == k, top, held[g][v] - below * top)
                    for h in range(g + 1, groups):
                        held[h][v] = held[h][v] - factor[h] * top
                yield
        for h in range(groups):
            for v in live:
                work[start + SUB * h:start + SUB * (h + 1), v * LANES:(v + 1) * LANES] = held[h][v]
        after = start + PANEL
        if after < order:
            base = (after // LANES) * LANES
            high, middle, low = split(work[start:after, base:])
            left = jnp.concatenate([high, high, middle, high, low, middle], axis=0)[:, :order - base]
            right = jnp.concatenate([high, middle, high, low, high, middle], axis=0)
            change = lax.dot_general(
                left, right, (((0,), (0,)), ((), ())), preferred_element_type=jnp.float32
            )
            work[after:, base:] = work[after:, base:] - change[after - base:]
        yield


def refresh_body(left_stat, left_basis, right_stat, right_basis, left_out, right_out, left_work, right_work):
    order = left_stat.shape[0]
    rows = lax.broadcasted_iota(jnp.int32, (SUB, LANES), 0)
    for stat, basis, work in ((left_stat, left_basis, left_work), (right_stat, right_basis, right_work)):
        powered_t = dot(basis[...], stat[...], 0, 0)
        work[:, order:] = powered_t
        work[:, :order] = dot(powered_t, powered_t, 1, 1)
    for _ in zip(eliminate(left_work, order, rows), eliminate(right_work, order, rows)):
        pass
    left_out[...] = left_work[:, order:].T
    right_out[...] = right_work[:, order:].T


def refresh(left_stat, left_basis, right_stat, right_basis):
    order = left_stat.shape[-1]
    result = jax.ShapeDtypeStruct((order, order), jnp.float32)
    return pl.pallas_call(
        refresh_body,
        out_shape=(result, result),
        scratch_shapes=[pltpu.VMEM((order, 2 * order), jnp.float32)] * 2,
        name="refresh",
    )(left_stat, left_basis, right_stat, right_basis)


def partner_pairs(size, step):
    if size & (size - 1):
        return [(at, (at + step) % size) for at in range(size)]
    return [(at, at ^ step) for at in range(size)]


def partner(at, size, step):
    return (at + step) % size if size & (size - 1) else at ^ step


def source(at, size, step):
    return (at - step) % size if size & (size - 1) else at ^ step


def swap(value, axis, size, step):
    return lax.ppermute(value, axis, partner_pairs(size, step))


def all_sum(value, sizes):
    for axis in sizes:
        size = sizes[axis]
        if size & (size - 1):
            value = lax.psum(value, axis)
            continue
        step = 1
        while step < size:
            value = value + swap(value, axis, size, step)
            step *= 2
    return value


def on_device(sizes, partials, momentum, second, left_stat, right_stat, left_basis, right_basis):
    tiles, order = left_basis.shape[:2]
    replicas = sizes["dp"]
    at = lax.axis_index("dp")
    replica_part = partials[0]
    row_count, shard_width = replica_part.shape
    col_bands = shard_width // order

    def corner(number):
        return (number // col_bands) * order, (number % col_bands) * order

    def chunk(owner):
        return jnp.stack([
            lax.dynamic_slice(replica_part, corner(owner * tiles + tile), (order, order))
            for tile in range(tiles)
        ])

    steps = sorted(range(1, replicas), key=lambda step: -step)
    received = [swap(chunk(partner(at, replicas, step)), "dp", replicas, step) for step in steps]
    gradient = chunk(at).astype(jnp.float32)
    for piece in received:
        gradient = gradient + piece.astype(jnp.float32)
    grad_local = jnp.sum(gradient * gradient)
    left_new = beta_second * left_stat + (1.0 - beta_second) * outer_right(gradient, gradient)
    right_new = beta_second * right_stat + (1.0 - beta_second) * inner_left(gradient, gradient)
    momentum_new = beta_first * momentum + (1.0 - beta_first) * gradient
    grad_rot = product(inner_left(left_basis, gradient), right_basis)
    moment_rot = product(inner_left(left_basis, momentum_new), right_basis)
    second_new = beta_second * second + (1.0 - beta_second) * grad_rot * grad_rot
    direction = moment_rot / (jnp.sqrt(second_new) + epsilon)
    step_local = jnp.sum(direction * direction)
    norms = all_sum(jnp.stack([grad_local, step_local]), sizes)
    raw_step = outer_right(product(left_basis, direction), right_basis)
    update = (raw_step * jnp.sqrt(norms[0] / norms[1])).astype(jnp.bfloat16)

    assembled = jnp.zeros((row_count, shard_width), jnp.bfloat16)

    def place(assembled, owner, value):
        for tile in range(tiles):
            assembled = lax.dynamic_update_slice(assembled, value[tile], corner(owner * tiles + tile))
        return assembled

    near = [(0, update)]
    if replicas & (replicas - 1) == 0 and replicas > 1:
        far = replicas // 2
        across = swap(update, "dp", replicas, far)
        parts = [(0, update), (far, across)]
        for base, value in ((0, update), (far, across)):
            for step in range(1, far):
                parts.append((base ^ step, swap(value, "dp", replicas, step)))
    else:
        parts = [(0, update)] + [(step, swap(update, "dp", replicas, step)) for step in range(1, replicas)]
    for step, value in parts:
        assembled = place(assembled, source(at, replicas, step), value)
    refreshed = [
        refresh(left_new[tile], left_basis[tile], right_new[tile], right_basis[tile])
        for tile in range(tiles)
    ]
    left_basis_new = jnp.stack([pair[0] for pair in refreshed])
    right_basis_new = jnp.stack([pair[1] for pair in refreshed])
    return (
        assembled,
        momentum_new,
        second_new,
        left_new,
        right_new,
        left_basis_new,
        right_basis_new,
    )


def solution(mesh):
    block = P(("dp", "mp"), None, None)
    sizes = dict(mesh.shape)

    def body(*arrays):
        return on_device(sizes, *arrays)

    return jax.shard_map(
        body,
        mesh=mesh,
        in_specs=(P("dp", None, "mp"),) + (block,) * 6,
        out_specs=(P(None, "mp"),) + (block,) * 6,
        check_vma=False,
    )
```

time: 268 us -> 92.1 us (0.34)
  other arithmetic: 111 us -> 5.81 us
  waiting for transfers between devices: 72.8 us -> 23.9 us
  blocking collectives: 39.9 us -> 0 us
  starting transfers between devices: 0.08 us -> 36.1 us
  between operations: 18.5 us -> 2.32 us
  Pallas kernels: 0 us -> 12.5 us
  local copies, waits for them, and re-layouts: 14.9 us -> 4.54 us
  matrix products: 10.3 us -> 6.61 us
    another operation x19 -> x1, other arithmetic: 108 us -> 1.37 us  [on_device(): norms = all_sum(jnp.stack([grad_local, step_local]), sizes)]
    reduce_scatter x1 -> x0, waiting for transfers between devices: 72.8 us -> none  [on_device(): lax.psum_scatter(stacked.astype(jnp.float32), 'dp', scatter_dimension=0,...]
    psum x1 -> x0, blocking collectives: 39.9 us -> none  [on_device(): grad_norm = lax.psum(grad_local, ('dp', 'mp'))]
    ppermute x0 -> x19, starting transfers between devices: none -> 36.1 us  [swap(): return lax.ppermute(value, axis, partner_pairs(size, step))]
    ppermute x0 -> x19, waiting for transfers between devices: none -> 23.9 us  [swap(): return lax.ppermute(value, axis, partner_pairs(size, step))]
    pallas_call x0 -> x1, Pallas kernels: none -> 12.5 us  [refresh(): pl.pallas_call(refresh_body, out_shape=(result, result), scratch_shapes=[...]
    another operation x19 -> x0, local copies, waits for them, and re-layouts: 8.15 us -> none  [the longest x15 8.1 us: refresh(): lax.linalg.triangular_solve(factor, powered, left_side=False, lower=True,...]
    unnamed x26 -> x18, local copies, waits for them, and re-layouts: 6.54 us -> 2.41 us
  transfers between devices with their start and end apart: 2 -> 19, of which waited for: 1 -> 13; matrix products, arithmetic and copies ran while one was open for 46% -> 3% of each run, Pallas kernels for 0% -> 14%
where the time goes in v1:
time: 92.1 us; the launch traced here: 91.8 us
  starting transfers between devices  36.1 us (39%)
  waiting for transfers between devices  23.9 us (26%)
  Pallas kernels  12.5 us (14%)
  matrix products  6.61 us (7%)
  other arithmetic  5.81 us (6%)
  local copies, waits for them, and re-layouts  4.54 us (5%)
  between operations  2.32 us (3%)
    ppermute x19, starting transfers between devices, swap(): return lax.ppermute(value, axis, partner_pairs(size, step))  36.1 us
    ppermute x19, waiting for transfers between devices, swap(): return lax.ppermute(value, axis, partner_pairs(size, step))  23.9 us
    pallas_call x1, Pallas kernels, refresh(): pl.pallas_call(refresh_body, out_shape=(result, result), scratch_shapes=[...  12.5 us
    add x5, other arithmetic, all_sum(): value = value + swap(value, axis, size, step)  2.74 us
    dot_general x3, matrix products, inner_left(): return jnp.einsum('tji,tjk->tik', left, right, precision=highest)  2.49 us
    unnamed x18, local copies, waits for them, and re-layouts  2.41 us
    dot_general x3, matrix products, product(): return jnp.einsum('tij,tjk->tik', left, right, precision=highest)  2.4 us
  transfers between devices with their start and end apart: 19, of which 13 were waited for; matrix products, arithmetic and copies ran while one was open for 3% of the time, Pallas kernels for 14%

profile of v1, /device:TPU:0, one launch (start us, length us, event | category | flops | bytes accessed | tf_op | source)
XLA Modules:
  0.0 91.8 jit_solution(9357290391978017824)
XLA Ops:
  0.8 1.3 %constant_dynamic-slice_fusion.6 = (bf16[1,256,256]{2,1,0:T(8,128)(2,1)S(1)}, bf16[1,256,256]{2,1,0:T(8,128)(2,1)S(1)}, bf16[1,256,256]{2,1,0:T(8,128)(2,1)S(1)}...) fusion(bf16[1,256,2048]{2,1,0:T(8,128)(2,1)} %param.7, ...), kind=kLoop, calls=%fused_computation.39 | loop fusion | bytes 1835036 | tf_op jit(solution)/shard_map/dynamic_slice | solution.py:168
  2.1 6.1 %collective-permute-start = (bf16[1,256,256]{2,1,0:T(8,128)(2,1)S(1)}, bf16[1,256,256]{2,1,0:T(8,128)(2,1)S(1)}, u32[]{:S(2)}, u32[]{:S(2)}) collective-permute-start(bf16[1,256,256]{2,1,0:T(8,128)(2,1)S(1)} %get-tuple-element.13), channel_id=1, source_target_pairs={{0,28},{4,24},{8,20},{12,16},{16,12},{20,8},{24,4},{28,0},{1,29},{... | collective-permute-start | bytes 393224 | tf_op jit(solution)/shard_map/ppermute | solution.py:139
  8.2 0.2 collective-permute-start.1
  8.4 0.8 collective-permute-start.2
  9.2 2.0 %collective-permute-start.3 = (bf16[1,256,256]{2,1,0:T(8,128)(2,1)S(1)}, bf16[1,256,256]{2,1,0:T(8,128)(2,1)S(1)}, u32[]{:S(2)}, u32[]{:S(2)}) collective-permute-start(bf16[1,256,256]{2,1,0:T(8,128)(2,1)S(1)} %get-tuple-element.15), channel_id=1, source_target_pairs={{0,16},{4,20},{8,24},{12,28},{16,0},{20,4},{24,8},{28,12},{1,17},{... | collective-permute-start | bytes 393224 | tf_op jit(solution)/shard_map/ppermute | solution.py:139
  11.2 2.3 %collective-permute-start.4 = (bf16[1,256,256]{2,1,0:T(8,128)(2,1)S(1)}, bf16[1,256,256]{2,1,0:T(8,128)(2,1)S(1)}, u32[]{:S(2)}, u32[]{:S(2)}) collective-permute-start(bf16[1,256,256]{2,1,0:T(8,128)(2,1)S(1)} %get-tuple-element.14), channel_id=1, source_target_pairs={{0,12},{4,8},{8,4},{12,0},{16,28},{20,24},{24,20},{28,16},{1,13},{... | collective-permute-start | bytes 393224 | tf_op jit(solution)/shard_map/ppermute | solution.py:139
  13.5 0.0 collective-permute-done
  13.5 10.4 %collective-permute-start.5 = (bf16[1,256,256]{2,1,0:T(8,128)(2,1)S(1)}, bf16[1,256,256]{2,1,0:T(8,128)(2,1)S(1)}, u32[]{:S(2)}, u32[]{:S(2)}) collective-permute-start(bf16[1,256,256]{2,1,0:T(8,128)(2,1)S(1)} %get-tuple-element.19), channel_id=1, source_target_pairs={{0,8},{4,12},{8,0},{12,4},{16,24},{20,28},{24,16},{28,20},{1,9},{5... | collective-permute-start | bytes 393224 | tf_op jit(solution)/shard_map/ppermute | solution.py:139
  23.9 0.0 collective-permute-done.1
  23.9 1.4 %collective-permute-start.6 = (bf16[1,256,256]{2,1,0:T(8,128)(2,1)S(1)}, bf16[1,256,256]{2,1,0:T(8,128)(2,1)S(1)}, u32[]{:S(2)}, u32[]{:S(2)}) collective-permute-start(bf16[1,256,256]{2,1,0:T(8,128)(2,1)S(1)} %get-tuple-element.18), channel_id=1, source_target_pairs={{0,4},{4,0},{8,12},{12,8},{16,20},{20,16},{24,28},{28,24},{1,5},{5... | collective-permute-start | bytes 393224 | tf_op jit(solution)/shard_map/ppermute | solution.py:139
  25.3 3.5 %collective-permute-done.2 = bf16[1,256,256]{2,1,0:T(8,128)(2,1)S(1)} collective-permute-done((bf16[1,256,256]{2,1,0:T(8,128)(2,1)S(1)}, bf16[1,256,256]{2,1,0:T(8,128)(2,1)S(1)}, u32[]{:S(2)}, u32[]{:S(2)}) %collective-permute-start.2) | collective-permute-done | bytes 131104 | tf_op jit(solution)/shard_map/ppermute | solution.py:139
  28.7 1.9 %collective-permute-done.3 = bf16[1,256,256]{2,1,0:T(8,128)(2,1)S(1)} collective-permute-done((bf16[1,256,256]{2,1,0:T(8,128)(2,1)S(1)}, bf16[1,256,256]{2,1,0:T(8,128)(2,1)S(1)}, u32[]{:S(2)}, u32[]{:S(2)}) %collective-permute-start.3) | collective-permute-done | bytes 131104 | tf_op jit(solution)/shard_map/ppermute | solution.py:139
  30.6 0.0 collective-permute-done.4
  30.6 1.1 %collective-permute-done.5 = bf16[1,256,256]{2,1,0:T(8,128)(2,1)S(1)} collective-permute-done((bf16[1,256,256]{2,1,0:T(8,128)(2,1)S(1)}, bf16[1,256,256]{2,1,0:T(8,128)(2,1)S(1)}, u32[]{:S(2)}, u32[]{:S(2)}) %collective-permute-start.5) | collective-permute-done | bytes 131104 | tf_op jit(solution)/shard_map/ppermute | solution.py:139
  31.7 0.0 collective-permute-done.6
  31.7 1.7 %multiply_reduce_fusion.1 = (f32[]{:T(128)}, f32[1,256,256]{2,1,0:T(8,128)S(1)}) fusion(bf16[1,256,256]{2,1,0:T(8,128)(2,1)S(1)} %collective-permute-done.6, bf16[1,256,256]{2,1,0:T(8,128)(2,1)S(1)} %collective-permute-done.5, bf16[1,256,256]{2,1,0:T(8,128)(2,1)S(1)} %collective-permute-done.4, bf16[1,256,256]{2,1,0:T(8,128)(2,1)S(1)} %collective-permute-done.3, ...), kind=kLoop, calls=%fused_computation.22 | loop fusion | flops 1114111 | bytes 1310728 | tf_op jit(solution)/shard_map/reduce_sum | solution.py:177
  33.4 0.0 copy-done.4
  33.5 0.9 copy-done
  34.4 0.6 fusion.12
  35.0 0.1 copy-done.2
  35.1 0.6 fusion.14
  35.7 0.3 copy-done.1
  36.0 0.1 copy-done.7
  36.1 0.6 fusion.7
  36.7 0.0 copy-start.8
  36.7 1.2 %multiply_reduce_fusion = (f32[]{:T(128)}, f32[1,256,256]{2,1,0:T(8,128)S(1)}) fusion(f32[1,256,256]{2,1,0:T(8,128)S(1)} %fusion.7, f32[256,256]{1,0:T(8,128)S(1)} %fusion.14, f32[1,256,256]{2,1,0:T(8,128)S(1)} %copy-done.1), kind=kOutput, calls=%fused_computation.21 | convolution fusion | flops 201588736 | bytes 1048580 | tf_op jit(solution)/shard_map/tij,tjk->tik/dot_general | solution.py:18
  37.9 0.0 copy-done.8
  37.9 0.6 fusion.8
  38.5 1.4 %pad_maximum_fusion = f32[2]{0:T(128)S(1)} fusion(f32[1]{0:T(128)} %bitcast.8, f32[1]{0:T(128)} %bitcast.7), kind=kLoop, calls=%fused_computation.40 | loop fusion | flops 2 | bytes 16 | tf_op jit(solution)/shard_map/stack | solution.py:186
  39.9 0.7 collective-permute-start.7
  40.6 1.1 %fusion.2 = f32[1,256,256]{2,1,0:T(8,128)} fusion(f32[1,256,256]{2,1,0:T(8,128)S(1)} %get-tuple-element.12, f32[1,256,256]{2,1,0:T(8,128)S(1)} %copy-done.5), kind=kOutput, calls=%fused_computation.6 | convolution fusion | flops 201523200 | bytes 786432 | tf_op jit(solution)/shard_map/tij,tkj->tik/dot_general | solution.py:26
  41.7 1.7 %collective-permute-done.7 = f32[2]{0:T(128)S(1)} collective-permute-done((f32[2]{0:T(128)S(1)}, f32[2]{0:T(128)S(1)}, u32[]{:S(2)}, u32[]{:S(2)}) %collective-permute-start.7) | collective-permute-done | bytes 40 | tf_op jit(solution)/shard_map/ppermute | solution.py:139
  43.5 1.4 %fusion.29 = f32[2]{0:T(128)S(1)} fusion(f32[2]{0:T(128)S(1)} %collective-permute-done.7, f32[1]{0:T(128)} %bitcast.8, f32[1]{0:T(128)} %bitcast.7), kind=kLoop, calls=%fused_computation.49 | loop fusion | flops 4 | bytes 24 | tf_op jit(solution)/shard_map/add | solution.py:150
  44.8 0.0 collective-permute-start.8
  44.9 3.6 %collective-permute-done.8 = f32[2]{0:T(128)S(1)} collective-permute-done((f32[2]{0:T(128)S(1)}, f32[2]{0:T(128)S(1)}, u32[]{:S(2)}, u32[]{:S(2)}) %collective-permute-start.8) | collective-permute-done | bytes 40 | tf_op jit(solution)/shard_map/ppermute | solution.py:139
  48.4 1.4 %fusion.30 = f32[2]{0:T(128)S(1)} fusion(f32[2]{0:T(128)S(1)} %collective-permute-done.8, f32[2]{0:T(128)S(1)} %collective-permute-done.7, f32[1]{0:T(128)} %bitcast.8, f32[1]{0:T(128)} %bitcast.7), kind=kLoop, calls=%fused_computation.50 | loop fusion | flops 6 | bytes 32 | tf_op jit(solution)/shard_map/add | solution.py:150
  49.8 0.8 collective-permute-start.9
  50.6 3.6 %collective-permute-done.9 = f32[2]{0:T(128)S(1)} collective-permute-done((f32[2]{0:T(128)S(1)}, f32[2]{0:T(128)S(1)}, u32[]{:S(2)}, u32[]{:S(2)}) %collective-permute-start.9) | collective-permute-done | bytes 40 | tf_op jit(solution)/shard_map/ppermute | solution.py:139
  54.3 0.0 collective-permute-start.10
  54.3 1.2 %collective-permute-done.10 = f32[2]{0:T(128)S(1)} collective-permute-done((f32[2]{0:T(128)S(1)}, f32[2]{0:T(128)S(1)}, u32[]{:S(2)}, u32[]{:S(2)}) %collective-permute-start.10) | collective-permute-done | bytes 40 | tf_op jit(solution)/shard_map/ppermute | solution.py:139
  55.4 1.5 %collective-permute-start.11 = (f32[2]{0:T(128)S(1)}, f32[2]{0:T(128)S(1)}, u32[]{:S(2)}, u32[]{:S(2)}) collective-permute-start(f32[2]{0:T(128)S(1)} %add.173), channel_id=1, source_target_pairs={{0,2},{1,3},{2,0},{3,1},{4,6},{5,7},{6,4},{7,5},{8,10},{9,11},{10,... | collective-permute-start | bytes 32 | tf_op jit(solution)/shard_map/ppermute | solution.py:139
  56.9 2.0 %collective-permute-done.11 = f32[2]{0:T(128)S(1)} collective-permute-done((f32[2]{0:T(128)S(1)}, f32[2]{0:T(128)S(1)}, u32[]{:S(2)}, u32[]{:S(2)}) %collective-permute-start.11) | collective-permute-done | bytes 40 | tf_op jit(solution)/shard_map/ppermute | solution.py:139
  59.0 0.6 fusion.25
  61.0 0.1 broadcast_in_dim.3
  61.1 0.0 copy-start.6
  61.1 0.6 constant_dynamic-update-slice_fusion
  61.7 0.9 collective-permute-start.12
  62.6 1.3 %fusion.3 = f32[1,256,256]{2,1,0:T(8,128)} fusion(f32[1,256,256]{2,1,0:T(8,128)S(1)} %get-tuple-element.12, f32[1,256,256]{2,1,0:T(8,128)S(1)} %copy-done.6), kind=kOutput, calls=%fused_computation.7 | convolution fusion | flops 201523200 | bytes 786432 | tf_op jit(solution)/shard_map/tji,tjk->tik/dot_general | solution.py:22
  63.9 12.5 %refresh.1 = (f32[256,256]{1,0:T(8,128)}, f32[256,256]{1,0:T(8,128)}) custom-call(f32[256,256]{1,0:T(8,128)} %bitcast.76, f32[256,256]{1,0:T(8,128)} %bitcast.74, f32[256,256]{1,0:T(8,128)} %bitcast.77, f32[256,256]{1,0:T(8,128)} %bitcast.75), custom_call_target="tpu_custom_call" | custom-call | tf_op jit(solution)/shard_map/refresh/pallas_call | solution.py:116
  76.4 0.9 collective-permute-start.13
  77.3 2.0 %collective-permute-start.14 = (bf16[1,256,256]{2,1,0:T(8,128)(2,1)S(1)}, bf16[1,256,256]{2,1,0:T(8,128)(2,1)S(1)}, u32[]{:S(2)}, u32[]{:S(2)}) collective-permute-start(bf16[1,256,256]{2,1,0:T(8,128)(2,1)S(1)} %bitcast.80), channel_id=1, source_target_pairs={{0,8},{4,12},{8,0},{12,4},{16,24},{20,28},{24,16},{28,20},{1,9},{5... | collective-permute-start | bytes 393224 | tf_op jit(solution)/shard_map/ppermute | solution.py:139
  79.3 0.6 collective-permute-start.15
  79.9 0.0 collective-permute-done.12
  79.9 0.9 collective-permute-start.16
  80.8 2.0 %collective-permute-start.17 = (bf16[1,256,256]{2,1,0:T(8,128)(2,1)S(1)}, bf16[1,256,256]{2,1,0:T(8,128)(2,1)S(1)}, u32[]{:S(2)}, u32[]{:S(2)}) collective-permute-start(bf16[1,256,256]{2,1,0:T(8,128)(2,1)S(1)} %collective-permute-done.12), channel_id=1, source_target_pairs={{0,8},{4,12},{8,0},{12,4},{16,24},{20,28},{24,16},{28,20},{1,9},{5... | collective-permute-start | bytes 393224 | tf_op jit(solution)/shard_map/ppermute | solution.py:139
  82.8 0.6 collective-permute-done.13
  83.5 2.6 %collective-permute-start.18 = (bf16[1,256,256]{2,1,0:T(8,128)(2,1)S(1)}, bf16[1,256,256]{2,1,0:T(8,128)(2,1)S(1)}, u32[]{:S(2)}, u32[]{:S(2)}) collective-permute-start(bf16[1,256,256]{2,1,0:T(8,128)(2,1)S(1)} %collective-permute-done.12), channel_id=1, source_target_pairs={{0,12},{4,8},{8,4},{12,0},{16,28},{20,24},{24,20},{28,16},{1,13},{... | collective-permute-start | bytes 393224 | tf_op jit(solution)/shard_map/ppermute | solution.py:139
  86.1 0.0 collective-permute-done.14
  86.2 1.0 %collective-permute-done.15 = bf16[1,256,256]{2,1,0:T(8,128)(2,1)S(1)} collective-permute-done((bf16[1,256,256]{2,1,0:T(8,128)(2,1)S(1)}, bf16[1,256,256]{2,1,0:T(8,128)(2,1)S(1)}, u32[]{:S(2)}, u32[]{:S(2)}) %collective-permute-start.15) | collective-permute-done | bytes 131104 | tf_op jit(solution)/shard_map/ppermute | solution.py:139
  87.2 0.6 collective-permute-done.16
  87.8 1.3 %collective-permute-done.17 = bf16[1,256,256]{2,1,0:T(8,128)(2,1)S(1)} collective-permute-done((bf16[1,256,256]{2,1,0:T(8,128)(2,1)S(1)}, bf16[1,256,256]{2,1,0:T(8,128)(2,1)S(1)}, u32[]{:S(2)}, u32[]{:S(2)}) %collective-permute-start.17) | collective-permute-done | bytes 131104 | tf_op jit(solution)/shard_map/ppermute | solution.py:139
  89.1 1.7 %collective-permute-done.18 = bf16[1,256,256]{2,1,0:T(8,128)(2,1)S(1)} collective-permute-done((bf16[1,256,256]{2,1,0:T(8,128)(2,1)S(1)}, bf16[1,256,256]{2,1,0:T(8,128)(2,1)S(1)}, u32[]{:S(2)}, u32[]{:S(2)}) %collective-permute-start.18) | collective-permute-done | bytes 131104 | tf_op jit(solution)/shard_map/ppermute | solution.py:139
  90.8 0.0 copy-start.3
  90.9 1.0 %copy-done.3 = bf16[256,2048]{1,0:T(8,128)(2,1)} copy-done((bf16[256,2048]{1,0:T(8,128)(2,1)}, bf16[256,2048]{1,0:T(8,128)(2,1)S(1)}, u32[]{:S(2)}) %copy-start.3) | copy-done | bytes 1048600
  (19 shorter events, 0.2 us)
Async XLA Ops:
  2.1 11.4 %collective-permute-start = (bf16[1,256,256]{2,1,0:T(8,128)(2,1)S(1)}, bf16[1,256,256]{2,1,0:T(8,128)(2,1)S(1)}, u32[]{:S(2)}, u32[]{:S(2)}) collective-permute-start(bf16[1,256,256]{2,1,0:T(8,128)(2,1)S(1)} %get-tuple-element.13), channel_id=1, source_target_pairs={{0,28},{4,24},{8,20},{12,16},{16,12},{20,8},{24,4},{28,0},{1,29},{... | collective-permute-start | bytes 393224 | tf_op jit(solution)/shard_map/ppermute | solution.py:139
  8.2 15.7 %collective-permute-start.1 = (bf16[1,256,256]{2,1,0:T(8,128)(2,1)S(1)}, bf16[1,256,256]{2,1,0:T(8,128)(2,1)S(1)}, u32[]{:S(2)}, u32[]{:S(2)}) collective-permute-start(bf16[1,256,256]{2,1,0:T(8,128)(2,1)S(1)} %get-tuple-element.17), channel_id=1, source_target_pairs={{0,24},{4,28},{8,16},{12,20},{16,8},{20,12},{24,0},{28,4},{1,25},{... | collective-permute-start | bytes 393224 | tf_op jit(solution)/shard_map/ppermute | solution.py:139
  8.4 20.3 %collective-permute-start.2 = (bf16[1,256,256]{2,1,0:T(8,128)(2,1)S(1)}, bf16[1,256,256]{2,1,0:T(8,128)(2,1)S(1)}, u32[]{:S(2)}, u32[]{:S(2)}) collective-permute-start(bf16[1,256,256]{2,1,0:T(8,128)(2,1)S(1)} %get-tuple-element.16), channel_id=1, source_target_pairs={{0,20},{4,16},{8,28},{12,24},{16,4},{20,0},{24,12},{28,8},{1,21},{... | collective-permute-start | bytes 393224 | tf_op jit(solution)/shard_map/ppermute | solution.py:139
  9.2 21.4 %collective-permute-start.3 = (bf16[1,256,256]{2,1,0:T(8,128)(2,1)S(1)}, bf16[1,256,256]{2,1,0:T(8,128)(2,1)S(1)}, u32[]{:S(2)}, u32[]{:S(2)}) collective-permute-start(bf16[1,256,256]{2,1,0:T(8,128)(2,1)S(1)} %get-tuple-element.15), channel_id=1, source_target_pairs={{0,16},{4,20},{8,24},{12,28},{16,0},{20,4},{24,8},{28,12},{1,17},{... | collective-permute-start | bytes 393224 | tf_op jit(solution)/shard_map/ppermute | solution.py:139
  11.2 19.4 %collective-permute-start.4 = (bf16[1,256,256]{2,1,0:T(8,128)(2,1)S(1)}, bf16[1,256,256]{2,1,0:T(8,128)(2,1)S(1)}, u32[]{:S(2)}, u32[]{:S(2)}) collective-permute-start(bf16[1,256,256]{2,1,0:T(8,128)(2,1)S(1)} %get-tuple-element.14), channel_id=1, source_target_pairs={{0,12},{4,8},{8,4},{12,0},{16,28},{20,24},{24,20},{28,16},{1,13},{... | collective-permute-start | bytes 393224 | tf_op jit(solution)/shard_map/ppermute | solution.py:139
  13.5 18.3 %collective-permute-start.5 = (bf16[1,256,256]{2,1,0:T(8,128)(2,1)S(1)}, bf16[1,256,256]{2,1,0:T(8,128)(2,1)S(1)}, u32[]{:S(2)}, u32[]{:S(2)}) collective-permute-start(bf16[1,256,256]{2,1,0:T(8,128)(2,1)S(1)} %get-tuple-element.19), channel_id=1, source_target_pairs={{0,8},{4,12},{8,0},{12,4},{16,24},{20,28},{24,16},{28,20},{1,9},{5... | collective-permute-start | bytes 393224 | tf_op jit(solution)/shard_map/ppermute | solution.py:139
  23.9 7.8 %collective-permute-start.6 = (bf16[1,256,256]{2,1,0:T(8,128)(2,1)S(1)}, bf16[1,256,256]{2,1,0:T(8,128)(2,1)S(1)}, u32[]{:S(2)}, u32[]{:S(2)}) collective-permute-start(bf16[1,256,256]{2,1,0:T(8,128)(2,1)S(1)} %get-tuple-element.18), channel_id=1, source_target_pairs={{0,4},{4,0},{8,12},{12,8},{16,20},{20,16},{24,28},{28,24},{1,5},{5... | collective-permute-start | bytes 393224 | tf_op jit(solution)/shard_map/ppermute | solution.py:139
  25.3 8.1 %copy-start.4 = (f32[1,256,256]{2,1,0:T(8,128)S(1)}, f32[1,256,256]{2,1,0:T(8,128)}, u32[]{:S(2)}) copy-start(f32[1,256,256]{2,1,0:T(8,128)} %param.8) | copy-start | bytes 786436
  33.4 1.0 %copy-start = (f32[1,256,256]{2,1,0:T(8,128)S(1)}, f32[1,256,256]{2,1,0:T(8,128)}, u32[]{:S(2)}) copy-start(f32[1,256,256]{2,1,0:T(8,128)} %param.12) | copy-start | bytes 786436
  34.4 0.7 copy-start.2
  35.1 0.9 %copy-start.1 = (f32[1,256,256]{2,1,0:T(8,128)S(1)}, f32[1,256,256]{2,1,0:T(8,128)}, u32[]{:S(2)}) copy-start(f32[1,256,256]{2,1,0:T(8,128)} %param.13) | copy-start | bytes 786436
  35.1 1.0 %copy-start.7 = (f32[1,256,256]{2,1,0:T(8,128)S(1)}, f32[1,256,256]{2,1,0:T(8,128)}, u32[]{:S(2)}) copy-start(f32[1,256,256]{2,1,0:T(8,128)} %param.9) | copy-start | bytes 786436
  36.7 1.2 %copy-start.8 = (f32[1,256,256]{2,1,0:T(8,128)}, f32[1,256,256]{2,1,0:T(8,128)S(1)}, u32[]{:S(2)}) copy-start(f32[1,256,256]{2,1,0:T(8,128)S(1)} %fusion.7) | copy-start | bytes 786436
  37.9 2.7 %copy-start.5 = (f32[1,256,256]{2,1,0:T(8,128)S(1)}, f32[1,256,256]{2,1,0:T(8,128)}, u32[]{:S(2)}) copy-start(f32[1,256,256]{2,1,0:T(8,128)} %param.10) | copy-start | bytes 786436
  39.9 3.6 %collective-permute-start.7 = (f32[2]{0:T(128)S(1)}, f32[2]{0:T(128)S(1)}, u32[]{:S(2)}, u32[]{:S(2)}) collective-permute-start(f32[2]{0:T(128)S(1)} %pad_maximum_fusion), channel_id=1, source_target_pairs={{0,4},{4,0},{8,12},{12,8},{16,20},{20,16},{24,28},{28,24},{1,5},{5... | collective-permute-start | bytes 32 | tf_op jit(solution)/shard_map/ppermute | solution.py:139
  44.8 3.6 %collective-permute-start.8 = (f32[2]{0:T(128)S(1)}, f32[2]{0:T(128)S(1)}, u32[]{:S(2)}, u32[]{:S(2)}) collective-permute-start(f32[2]{0:T(128)S(1)} %fusion.29), channel_id=1, source_target_pairs={{0,8},{4,12},{8,0},{12,4},{16,24},{20,28},{24,16},{28,20},{1,9},{5... | collective-permute-start | bytes 32 | tf_op jit(solution)/shard_map/ppermute | solution.py:139
  49.8 4.5 %collective-permute-start.9 = (f32[2]{0:T(128)S(1)}, f32[2]{0:T(128)S(1)}, u32[]{:S(2)}, u32[]{:S(2)}) collective-permute-start(f32[2]{0:T(128)S(1)} %fusion.30), channel_id=1, source_target_pairs={{0,16},{4,20},{8,24},{12,28},{16,0},{20,4},{24,8},{28,12},{1,17},{... | collective-permute-start | bytes 32 | tf_op jit(solution)/shard_map/ppermute | solution.py:139
  54.3 1.2 %collective-permute-start.10 = (f32[2]{0:T(128)S(1)}, f32[2]{0:T(128)S(1)}, u32[]{:S(2)}, u32[]{:S(2)}) collective-permute-start(f32[2]{0:T(128)S(1)} %add.172), channel_id=1, source_target_pairs={{0,1},{1,0},{2,3},{3,2},{4,5},{5,4},{6,7},{7,6},{8,9},{9,8},{10,11... | collective-permute-start | bytes 32 | tf_op jit(solution)/shard_map/ppermute | solution.py:139
  55.4 3.6 %collective-permute-start.11 = (f32[2]{0:T(128)S(1)}, f32[2]{0:T(128)S(1)}, u32[]{:S(2)}, u32[]{:S(2)}) collective-permute-start(f32[2]{0:T(128)S(1)} %add.173), channel_id=1, source_target_pairs={{0,2},{1,3},{2,0},{3,1},{4,6},{5,7},{6,4},{7,5},{8,10},{9,11},{10,... | collective-permute-start | bytes 32 | tf_op jit(solution)/shard_map/ppermute | solution.py:139
  61.1 1.5 %copy-start.6 = (f32[1,256,256]{2,1,0:T(8,128)S(1)}, f32[1,256,256]{2,1,0:T(8,128)}, u32[]{:S(2)}) copy-start(f32[1,256,256]{2,1,0:T(8,128)} %param.11) | copy-start | bytes 786436
  61.7 18.2 %collective-permute-start.12 = (bf16[1,256,256]{2,1,0:T(8,128)(2,1)S(1)}, bf16[1,256,256]{2,1,0:T(8,128)(2,1)S(1)}, u32[]{:S(2)}, u32[]{:S(2)}) collective-permute-start(bf16[1,256,256]{2,1,0:T(8,128)(2,1)S(1)} %bitcast.78), channel_id=1, source_target_pairs={{0,16},{4,20},{8,24},{12,28},{16,0},{20,4},{24,8},{28,12},{1,17},{... | collective-permute-start | bytes 393224 | tf_op jit(solution)/shard_map/ppermute | solution.py:139
  76.4 7.1 %collective-permute-start.13 = (bf16[1,256,256]{2,1,0:T(8,128)(2,1)S(1)}, bf16[1,256,256]{2,1,0:T(8,128)(2,1)S(1)}, u32[]{:S(2)}, u32[]{:S(2)}) collective-permute-start(bf16[1,256,256]{2,1,0:T(8,128)(2,1)S(1)} %bitcast.79), channel_id=1, source_target_pairs={{0,4},{4,0},{8,12},{12,8},{16,20},{20,16},{24,28},{28,24},{1,5},{5... | collective-permute-start | bytes 393224 | tf_op jit(solution)/shard_map/ppermute | solution.py:139
  77.3 8.8 %collective-permute-start.14 = (bf16[1,256,256]{2,1,0:T(8,128)(2,1)S(1)}, bf16[1,256,256]{2,1,0:T(8,128)(2,1)S(1)}, u32[]{:S(2)}, u32[]{:S(2)}) collective-permute-start(bf16[1,256,256]{2,1,0:T(8,128)(2,1)S(1)} %bitcast.80), channel_id=1, source_target_pairs={{0,8},{4,12},{8,0},{12,4},{16,24},{20,28},{24,16},{28,20},{1,9},{5... | collective-permute-start | bytes 393224 | tf_op jit(solution)/shard_map/ppermute | solution.py:139
  79.3 7.8 %collective-permute-start.15 = (bf16[1,256,256]{2,1,0:T(8,128)(2,1)S(1)}, bf16[1,256,256]{2,1,0:T(8,128)(2,1)S(1)}, u32[]{:S(2)}, u32[]{:S(2)}) collective-permute-start(bf16[1,256,256]{2,1,0:T(8,128)(2,1)S(1)} %bitcast.81), channel_id=1, source_target_pairs={{0,12},{4,8},{8,4},{12,0},{16,28},{20,24},{24,20},{28,16},{1,13},{... | collective-permute-start | bytes 393224 | tf_op jit(solution)/shard_map/ppermute | solution.py:139
  79.9 7.9 %collective-permute-start.16 = (bf16[1,256,256]{2,1,0:T(8,128)(2,1)S(1)}, bf16[1,256,256]{2,1,0:T(8,128)(2,1)S(1)}, u32[]{:S(2)}, u32[]{:S(2)}) collective-permute-start(bf16[1,256,256]{2,1,0:T(8,128)(2,1)S(1)} %collective-permute-done.12), channel_id=1, source_target_pairs={{0,4},{4,0},{8,12},{12,8},{16,20},{20,16},{24,28},{28,24},{1,5},{5... | collective-permute-start | bytes 393224 | tf_op jit(solution)/shard_map/ppermute | solution.py:139
  80.8 8.3 %collective-permute-start.17 = (bf16[1,256,256]{2,1,0:T(8,128)(2,1)S(1)}, bf16[1,256,256]{2,1,0:T(8,128)(2,1)S(1)}, u32[]{:S(2)}, u32[]{:S(2)}) collective-permute-start(bf16[1,256,256]{2,1,0:T(8,128)(2,1)S(1)} %collective-permute-done.12), channel_id=1, source_target_pairs={{0,8},{4,12},{8,0},{12,4},{16,24},{20,28},{24,16},{28,20},{1,9},{5... | collective-permute-start | bytes 393224 | tf_op jit(solution)/shard_map/ppermute | solution.py:139
  83.5 7.4 %collective-permute-start.18 = (bf16[1,256,256]{2,1,0:T(8,128)(2,1)S(1)}, bf16[1,256,256]{2,1,0:T(8,128)(2,1)S(1)}, u32[]{:S(2)}, u32[]{:S(2)}) collective-permute-start(bf16[1,256,256]{2,1,0:T(8,128)(2,1)S(1)} %collective-permute-done.12), channel_id=1, source_target_pairs={{0,12},{4,8},{8,4},{12,0},{16,28},{20,24},{24,20},{28,16},{1,13},{... | collective-permute-start | bytes 393224 | tf_op jit(solution)/shard_map/ppermute | solution.py:139
  90.8 1.0 %copy-start.3 = (bf16[256,2048]{1,0:T(8,128)(2,1)}, bf16[256,2048]{1,0:T(8,128)(2,1)S(1)}, u32[]{:S(2)}) copy-start(bf16[256,2048]{1,0:T(8,128)(2,1)S(1)} %bitcast_dynamic-update-slice_fusion) | copy-start | bytes 3145732

commit v2 on v1

v2 whole, which is shorter than its diff:
```python
import jax
import jax.numpy as jnp
from jax import lax
from jax.experimental import pallas as pl
from jax.experimental.pallas import tpu as pltpu
from jax.sharding import PartitionSpec as P


beta_first = 0.9
beta_second = 0.95
epsilon = 1e-08
highest = lax.Precision.HIGHEST
SUB = 8
LANES = 128
PANEL = 32
KERNEL_BYTES = 16 * 2**20


def dot(left, right, left_dim, right_dim):
    return lax.dot_general(
        left,
        right,
        (((left_dim,), (right_dim,)), ((), ())),
        precision=highest,
        preferred_element_type=jnp.float32,
    )


def split(value):
    high = value.astype(jnp.bfloat16)
    rest = value - high.astype(jnp.float32)
    middle = rest.astype(jnp.bfloat16)
    low = (rest - middle.astype(jnp.float32)).astype(jnp.bfloat16)
    return high, middle, low


def lane(value, at):
    return jnp.broadcast_to(value[:, at:at + 1], (SUB, LANES))


def row(value, at):
    return jnp.broadcast_to(value[at:at + 1, :], (SUB, LANES))


def eliminate(work, order, rows):
    tiles = 2 * order // LANES
    groups = PANEL // SUB
    for start in range(0, order, PANEL):
        first = start // LANES
        live = range(first, tiles)
        held = [
            {v: work[start + SUB * h:start + SUB * (h + 1), v * LANES:(v + 1) * LANES] for v in live}
            for h in range(groups)
        ]
        for g in range(groups):
            at = (start + SUB * g) % LANES
            cols = {h: [lane(held[h][first], at + k) for k in range(SUB)] for h in range(g, groups)}
            yield
            for k in range(SUB):
                inverse = lax.rsqrt(row(cols[g][k], k))
                factor = {h: cols[h][k] * inverse for h in range(g, groups)}
                below = jnp.where(rows > k, factor[g], 0.0)
                for l in range(k + 1, SUB):
                    pivot = row(factor[g], l)
                    cols[g][l] = cols[g][l] - below * pivot
                    for h in range(g + 1, groups):
                        cols[h][l] = cols[h][l] - factor[h] * pivot
                for v in live:
                    top = row(held[g][v], k) * inverse
                    held[g][v] = jnp.where(rows == k, top, held[g][v] - below * top)
                    for h in range(g + 1, groups):
                        held[h][v] = held[h][v] - factor[h] * top
                yield
        for h in range(groups):
            for v in live:
                work[start + SUB * h:start + SUB * (h + 1), v * LANES:(v + 1) * LANES] = held[h][v]
        after = start + PANEL
        if after < order:
            base = (after // LANES) * LANES
            high, middle, low = split(work[start:after, base:])
            left = jnp.concatenate([high, high, middle, high, low, middle], axis=0)[:, :order - base]
            right = jnp.concatenate([high, middle, high, low, high, middle], axis=0)
            change = lax.dot_general(
                left, right, (((0,), (0,)), ((), ())), preferred_element_type=jnp.float32
            )
            work[after:, base:] = work[after:, base:] - change[after - base:]
        yield


def in_vmem(value):
    return pltpu.with_memory_space_constraint(value, pltpu.VMEM)


def local_call(body, outs, args, flops, scratch=()):
    whole = pl.BlockSpec(memory_space=pltpu.VMEM)
    return pl.pallas_call(
        body,
        out_shape=tuple(pltpu.VMEM(shape, dtype) for shape, dtype in outs),
        in_specs=[whole] * len(args),
        out_specs=(whole,) * len(outs),
        scratch_shapes=list(scratch),
        cost_estimate=pl.CostEstimate(flops=flops, transcendentals=0, bytes_accessed=0),
        compiler_params=pltpu.CompilerParams(vmem_limit_bytes=KERNEL_BYTES),
    )(*[in_vmem(value) for value in args])


def total(refs):
    value = refs[0][0].astype(jnp.float32)
    for ref in refs[1:]:
        value = value + ref[0].astype(jnp.float32)
    return value


def add_pieces(pieces):
    def body(*refs):
        refs[-1][0] = total(refs[:-1])

    return local_call(body, [(pieces[0].shape, jnp.float32)], pieces, 10**6)[0]


def square_sum(value):
    return jnp.sum(value * value, axis=0, keepdims=True)


def rotate(pieces, momentum, second, left_basis, right_basis):
    count = len(pieces)

    def body(*refs):
        momentum_ref, second_ref, left_ref, right_ref = refs[count:count + 4]
        grad_out, momentum_out, second_out, direction_out, norm_out = refs[count + 4:]
        order = left_ref.shape[1]
        gradient = total(refs[:count])
        grad_out[0] = gradient
        moment = beta_first * momentum_ref[0] + (1.0 - beta_first) * gradient
        momentum_out[0] = moment
        right = right_ref[0]
        turned = dot(left_ref[0], jnp.concatenate([gradient, moment], axis=1), 0, 0)
        grad_rot = dot(turned[:, :order], right, 1, 0)
        moment_rot = dot(turned[:, order:], right, 1, 0)
        second_new = beta_second * second_ref[0] + (1.0 - beta_second) * grad_rot * grad_rot
        second_out[0] = second_new
        direction = moment_rot / (jnp.sqrt(second_new) + epsilon)
        direction_out[0] = direction
        sums = jnp.concatenate([square_sum(gradient), square_sum(direction)], axis=0)
        norm_out[...] = jnp.broadcast_to(jnp.sum(sums, axis=1, keepdims=True), norm_out.shape)

    whole = (momentum.shape, jnp.float32)
    return local_call(
        body, [whole] * 4 + [((2, LANES), jnp.float32)],
        [*pieces, momentum, second, left_basis, right_basis], 3 * 10**8,
    )


def rotate_back(direction, left_basis, right_basis):
    def body(direction_ref, left_ref, right_ref, out):
        out[0] = dot(dot(left_ref[0], direction_ref[0], 1, 0), right_ref[0], 1, 1)

    return local_call(
        body, [(direction.shape, jnp.float32)],
        [direction, left_basis, right_basis], 10**8,
    )[0]


def scale_steps(norms, steps):
    def body(norm_ref, *refs):
        norm = norm_ref[...]
        factor = jnp.sqrt(norm[0:1, :] / norm[1:2, :])
        for at, ref in enumerate(refs[:-1]):
            for tile in range(0, ref.shape[2], LANES):
                part = ref[0, :, tile:tile + LANES] * factor
                refs[-1][at, :, tile:tile + LANES] = part.astype(jnp.bfloat16)

    shape = (len(steps),) + steps[0].shape[1:]
    return local_call(body, [(shape, jnp.bfloat16)], [norms, *steps], 10**6)[0]


def refresh_body(grad_ref, momentum_ref, second_ref, left_stat, left_basis, right_stat, right_basis,
                 momentum_out, second_out, left_out, right_out, left_basis_out, right_basis_out,
                 left_new, right_new, left_turned, right_turned, left_work, right_work, sems):
    order = left_stat.shape[1]
    rows = lax.broadcasted_iota(jnp.int32, (SUB, LANES), 0)
    copies = []

    def write(source, target):
        copies.append(pltpu.make_async_copy(source, target, sems.at[len(copies)]))
        copies[-1].start()

    write(momentum_ref, momentum_out)
    write(second_ref, second_out)
    gradient = grad_ref[0]
    left_new[0] = beta_second * left_stat[0] + (1.0 - beta_second) * dot(gradient, gradient, 1, 1)
    write(left_new, left_out)
    right_new[0] = beta_second * right_stat[0] + (1.0 - beta_second) * dot(gradient, gradient, 0, 0)
    write(right_new, right_out)
    for stat, basis, work in ((left_new, left_basis, left_work), (right_new, right_basis, right_work)):
        powered_t = dot(basis[0], stat[0], 0, 0)
        work[:, order:] = powered_t
        work[:, :order] = dot(powered_t, powered_t, 1, 1)
    for _ in zip(eliminate(left_work, order, rows), eliminate(right_work, order, rows)):
        pass
    left_turned[0] = left_work[:, order:].T
    write(left_turned, left_basis_out)
    right_turned[0] = right_work[:, order:].T
    write(right_turned, right_basis_out)
    for copy in copies:
        copy.wait()


def refresh(gradient, momentum_new, second_new, left_stat, left_basis, right_stat, right_basis):
    shape = left_stat.shape
    order = shape[-1]
    args = [gradient, momentum_new, second_new, left_stat, left_basis, right_stat, right_basis]
    block = pltpu.VMEM(shape, jnp.float32)
    work = pltpu.VMEM((order, 2 * order), jnp.float32)
    return pl.pallas_call(
        refresh_body,
        out_shape=(jax.ShapeDtypeStruct(shape, jnp.float32),) * 6,
        in_specs=[pl.BlockSpec(memory_space=pltpu.VMEM)] * len(args),
        out_specs=(pl.BlockSpec(memory_space=pl.ANY),) * 6,
        scratch_shapes=[block] * 4 + [work] * 2 + [pltpu.SemaphoreType.DMA((6,))],
        cost_estimate=pl.CostEstimate(flops=2 * 10**9, transcendentals=0, bytes_accessed=0),
        compiler_params=pltpu.CompilerParams(vmem_limit_bytes=KERNEL_BYTES),
        name="refresh",
    )(*[in_vmem(value) for value in args])


def assemble(at, gathered, far, row_count, shard_width):
    order = gathered[0][1].shape[-1]
    col_bands = shard_width // order
    steps = [step for step, _ in gathered]

    def body(at_ref, *refs):
        out, sems = refs[-2:]
        copies = []
        for step, ref in zip(steps, refs):
            for place in range(2):
                number = at_ref[0] ^ (step ^ (place * far))
                band = lax.div(number, jnp.int32(col_bands))
                top = pl.multiple_of(band * order, order)
                edge = pl.multiple_of((number - band * col_bands) * order, order)
                copies.append(pltpu.make_async_copy(
                    ref.at[place],
                    out.at[pl.ds(top, order), pl.ds(edge, order)],
                    sems.at[len(copies)],
                ))
                copies[-1].start()
        for copy in copies:
            copy.wait()

    whole = pl.BlockSpec(memory_space=pltpu.VMEM)
    return pl.pallas_call(
        body,
        out_shape=jax.ShapeDtypeStruct((row_count, shard_width), jnp.bfloat16),
        in_specs=[pl.BlockSpec(memory_space=pltpu.SMEM)] + [whole] * len(gathered),
        out_specs=pl.BlockSpec(memory_space=pl.ANY),
        scratch_shapes=[pltpu.SemaphoreType.DMA((2 * len(gathered),))],
        cost_estimate=pl.CostEstimate(flops=10**6, transcendentals=0, bytes_accessed=0),
        compiler_params=pltpu.CompilerParams(vmem_limit_bytes=KERNEL_BYTES),
        name="assemble",
    )(jnp.reshape(at, (1,)), *[in_vmem(value) for _, value in gathered])


def swap(value, axis, size, step):
    pairs = [(at, at ^ step) for at in range(size)]
    return lax.ppermute(value, axis, pairs)


def all_sum(value, sizes):
    for axis in sizes:
        step = 1
        while step < sizes[axis]:
            value = value + swap(value, axis, sizes[axis], step)
            step *= 2
    return value


def on_device(sizes, partials, momentum, second, left_stat, right_stat, left_basis, right_basis):
    order = left_basis.shape[1]
    replicas = sizes["dp"]
    far = replicas // 2
    near = range(1, far)
    at = lax.axis_index("dp")
    replica_part = partials[0]
    row_count, shard_width = replica_part.shape
    col_bands = shard_width // order

    def corner(number):
        row_band = lax.div(number, jnp.int32(col_bands))
        return row_band * order, (number - row_band * col_bands) * order

    def chunk(step):
        return lax.dynamic_slice(source, corner(at ^ step), (order, order))[None]

    source = replica_part

    first = [swap(chunk(far ^ step), "dp", replicas, step) for step in near]
    source = lax.optimization_barrier(replica_part)
    half = add_pieces([chunk(far)] + first)
    across = swap(half, "dp", replicas, far)
    second_hop = [swap(chunk(step), "dp", replicas, step) for step in near]
    gradient, momentum_new, second_new, direction, norm_local = rotate(
        [chunk(0)] + second_hop + [across], momentum, second, left_basis, right_basis
    )
    norms = all_sum(norm_local, sizes)
    raw_step = rotate_back(direction, left_basis, right_basis)
    raw_across = swap(raw_step, "dp", replicas, far)
    pair = scale_steps(norms, [raw_step, raw_across])
    gathered = [(0, pair)] + [(step, swap(pair, "dp", replicas, step)) for step in near]
    assembled = assemble(at, gathered, far, row_count, shard_width)
    momentum_new, second_new, left_new, right_new, left_basis_new, right_basis_new = refresh(
        gradient, momentum_new, second_new, left_stat, left_basis, right_stat, right_basis
    )
    return (
        assembled,
        momentum_new,
        second_new,
        left_new,
        right_new,
        left_basis_new,
        right_basis_new,
    )


def solution(mesh):
    block = P(("dp", "mp"), None, None)
    sizes = dict(mesh.shape)

    def body(*arrays):
        return on_device(sizes, *arrays)

    return jax.shard_map(
        body,
        mesh=mesh,
        in_specs=(P("dp", None, "mp"),) + (block,) * 6,
        out_specs=(P(None, "mp"),) + (block,) * 6,
        check_vma=False,
    )
```

time: 92.1 us -> 65.5 us (0.71)
  starting transfers between devices: 36.1 us -> 22.8 us
  matrix products: 6.61 us -> 0 us
  other arithmetic: 5.81 us -> 0.02 us
  Pallas kernels: 12.5 us -> 15.4 us
  local copies, waits for them, and re-layouts: 4.54 us -> 2.34 us
  between operations: 2.32 us -> 0.79 us
    ppermute x19 -> x16, starting transfers between devices: 36.1 us -> 22.8 us  [swap(): return lax.ppermute(value, axis, pairs)]
    dot_general x8 -> x0, matrix products: 6.61 us -> none  [the longest x3 2.49 us: inner_left(): return jnp.einsum('tji,tjk->tik', left, right, precision=highest)]
    pallas_call x1 -> x6, Pallas kernels: 12.5 us -> 15.4 us  [the longest x1 11.8 us: refresh(): pl.pallas_call(refresh_body, out_shape=(jax.ShapeDtypeStruct(shape, jnp.f...]
    add x6 -> x5, other arithmetic: 2.79 us -> 0.02 us  [all_sum(): value = value + swap(value, axis, sizes[axis], step)]
    unnamed x18 -> x12, local copies, waits for them, and re-layouts: 2.41 us -> 0.02 us
    reduce_sum x1 -> x0, other arithmetic: 1.66 us -> none  [on_device(): grad_local = jnp.sum(gradient * gradient)]
    another operation x1 -> x0, other arithmetic: 1.37 us -> none  [on_device(): norms = all_sum(jnp.stack([grad_local, step_local]), sizes)]
    broadcast_in_dim x1, local copies, waits for them, and re-layouts: 0.11 us -> 1.25 us  [chunk(): return lax.dynamic_slice(source, corner(at ^ step), (order, order))[None]]
  transfers between devices with their start and end apart: 19 -> 16, of which waited for: 13 -> 10; matrix products, arithmetic and copies ran while one was open for 3% -> 2% of each run, Pallas kernels for 14% -> 18%
where the time goes in v2:
time: 65.5 us; the launch traced here: 65.4 us
  waiting for transfers between devices  24 us (37%)
  starting transfers between devices  22.8 us (35%)
  Pallas kernels  15.4 us (24%)
  local copies, waits for them, and re-layouts  2.34 us (4%)
  between operations  0.79 us (1%)
    ppermute x16, waiting for transfers between devices, swap(): return lax.ppermute(value, axis, pairs)  24 us
    ppermute x16, starting transfers between devices, swap(): return lax.ppermute(value, axis, pairs)  22.8 us
    pallas_call x1, Pallas kernels, refresh(): pl.pallas_call(refresh_body, out_shape=(jax.ShapeDtypeStruct(shape, jnp.f...  11.8 us
    pallas_call x4, Pallas kernels, local_call(): pl.pallas_call(body, out_shape=tuple((pltpu.VMEM(shape, dtype) for shape,...  2.54 us
  transfers between devices with their start and end apart: 16, of which 10 were waited for; matrix products, arithmetic and copies ran while one was open for 2% of the time, Pallas kernels for 18%

profile of v2, /device:TPU:0, one launch (start us, length us, event | category | flops | bytes accessed | tf_op | source)
XLA Modules:
  0.0 65.4 jit_solution(16100228765543984197)
XLA Ops:
  0.7 1.1 %constant_dynamic-slice_fusion = (bf16[1,256,256]{2,1,0:T(8,128)(2,1)S(1)}, bf16[1,256,256]{2,1,0:T(8,128)(2,1)S(1)}, bf16[1,256,256]{2,1,0:T(8,128)(2,1)S(1)}) fusion(bf16[1,256,2048]{2,1,0:T(8,128)(2,1)} %param.7, s32[]{:T(128)S(6)} %select_n.39, s32[]{:T(128)S(6)} %select_n.37, s32[]{:T(128)S(6)} %select_n.38), kind=kLoop, calls=%fused_computation.5 | loop fusion | bytes 786444 | tf_op jit(solution)/shard_map/dynamic_slice | solution.py:292
  1.8 4.0 %collective-permute-start.5 = (bf16[1,256,256]{2,1,0:T(8,128)(2,1)S(1)}, bf16[1,256,256]{2,1,0:T(8,128)(2,1)S(1)}, u32[]{:S(2)}, u32[]{:S(2)}) collective-permute-start(bf16[1,256,256]{2,1,0:T(8,128)(2,1)S(1)} %get-tuple-element.29), channel_id=1, source_target_pairs={{0,12},{4,8},{8,4},{12,0},{16,28},{20,24},{24,20},{28,16},{1,13},{... | collective-permute-start | bytes 393224 | tf_op jit(solution)/shard_map/ppermute | solution.py:265
  5.8 0.5 collective-permute-start.3
  6.3 0.1 collective-permute-start.4
  6.4 0.0 copy-start.3
  6.4 1.3 %dynamic-slice_bitcast_fusion = (bf16[1,256,256]{2,1,0:T(8,128)(2,1)S(1)}, bf16[1,256,256]{2,1,0:T(8,128)(2,1)S(1)}, bf16[1,256,256]{2,1,0:T(8,128)(2,1)S(1)}, b...) fusion(bf16[256,2048]{1,0:T(8,128)(2,1)} %bitcast.12, s32[]{:T(128)S(6)} %select_n.36, s32[]{:T(128)S(6)} %select_n.35, ...), kind=kLoop, calls=%fused_computation | loop fusion | bytes 1310740 | tf_op jit(solution)/shard_map/broadcast_in_dim | solution.py:292
  7.7 2.0 %collective-permute-done.5.refs_3_ = bf16[1,256,256]{2,1,0:T(8,128)(2,1)S(1)} collective-permute-done((bf16[1,256,256]{2,1,0:T(8,128)(2,1)S(1)}, bf16[1,256,256]{2,1,0:T(8,128)(2,1)S(1)}, u32[]{:S(2)}, u32[]{:S(2)}) %collective-permute-start.5) | collective-permute-done | bytes 131104 | tf_op jit(solution)/shard_map/ppermute | solution.py:265
  9.7 2.4 %collective-permute-done.3.refs_1_ = bf16[1,256,256]{2,1,0:T(8,128)(2,1)S(1)} collective-permute-done((bf16[1,256,256]{2,1,0:T(8,128)(2,1)S(1)}, bf16[1,256,256]{2,1,0:T(8,128)(2,1)S(1)}, u32[]{:S(2)}, u32[]{:S(2)}) %collective-permute-start.3) | collective-permute-done | bytes 131104 | tf_op jit(solution)/shard_map/ppermute | solution.py:265
  12.1 0.2 collective-permute-done.4.refs_2_
  12.3 0.0 copy-start
  12.3 0.0 copy-start.1
  12.3 0.0 copy-start.2
  12.3 0.1 shard_map.126
  12.3 2.7 %collective-permute-start.6 = (f32[1,256,256]{2,1,0:T(8,128)S(1)}, f32[1,256,256]{2,1,0:T(8,128)S(1)}, u32[]{:S(2)}, u32[]{:S(2)}) collective-permute-start(f32[1,256,256]{2,1,0:T(8,128)S(1)} %shard_map.126), channel_id=1, source_target_pairs={{0,16},{4,20},{8,24},{12,28},{16,0},{20,4},{24,8},{28,12},{1,17},{... | collective-permute-start | bytes 786440 | tf_op jit(solution)/shard_map/ppermute | solution.py:265
  15.0 1.7 %collective-permute-start.2 = (bf16[1,256,256]{2,1,0:T(8,128)(2,1)S(1)}, bf16[1,256,256]{2,1,0:T(8,128)(2,1)S(1)}, u32[]{:S(2)}, u32[]{:S(2)}) collective-permute-start(bf16[1,256,256]{2,1,0:T(8,128)(2,1)S(1)} %get-tuple-element.33), channel_id=1, source_target_pairs={{0,12},{4,8},{8,4},{12,0},{16,28},{20,24},{24,20},{28,16},{1,13},{... | collective-permute-start | bytes 393224 | tf_op jit(solution)/shard_map/ppermute | solution.py:265
  16.7 1.2 %collective-permute-start.1 = (bf16[1,256,256]{2,1,0:T(8,128)(2,1)S(1)}, bf16[1,256,256]{2,1,0:T(8,128)(2,1)S(1)}, u32[]{:S(2)}, u32[]{:S(2)}) collective-permute-start(bf16[1,256,256]{2,1,0:T(8,128)(2,1)S(1)} %get-tuple-element.34), channel_id=1, source_target_pairs={{0,8},{4,12},{8,0},{12,4},{16,24},{20,28},{24,16},{28,20},{1,9},{5... | collective-permute-start | bytes 393224 | tf_op jit(solution)/shard_map/ppermute | solution.py:265
  17.9 0.5 collective-permute-start
  18.5 9.3 %collective-permute-done.2.refs_3_ = bf16[1,256,256]{2,1,0:T(8,128)(2,1)S(1)} collective-permute-done((bf16[1,256,256]{2,1,0:T(8,128)(2,1)S(1)}, bf16[1,256,256]{2,1,0:T(8,128)(2,1)S(1)}, u32[]{:S(2)}, u32[]{:S(2)}) %collective-permute-start.2) | collective-permute-done | bytes 131104 | tf_op jit(solution)/shard_map/ppermute | solution.py:265
  27.8 0.5 collective-permute-done.1.refs_2_
  28.3 0.0 collective-permute-done.refs_1_
  28.3 0.0 collective-permute-done.6.refs_4_
  28.3 0.0 copy-done.3
  28.3 0.0 copy-done
  28.3 0.0 copy-done.1
  28.3 0.0 copy-done.2
  28.3 1.4 %shard_map.127 = (f32[1,256,256]{2,1,0:T(8,128)S(1)}, f32[1,256,256]{2,1,0:T(8,128)S(1)}, f32[1,256,256]{2,1,0:T(8,128)S(1)}, f32[1,256,256]{2,1,0:T(8,128)S(1)}, f32[2,128]{1,0:T(2,128)S(1)}) custom-call(bf16[1,256,256]{2,1,0:T(8,128)(2,1)S(1)} %get-tuple-element.36.refs_0_, bf16[1,256,256]{2,1,0:T(8,128)(2,1)S(1)} %collective-permute-done.refs_1_, ...), custom_call_target="tpu_custom_call" | custom-call | flops 300000000 | tf_op jit(solution)/shard_map/pallas_call | solution.py:96
  29.7 1.0 %shard_map.128.refs_0_ = f32[1,256,256]{2,1,0:T(8,128)S(1)} custom-call(f32[1,256,256]{2,1,0:T(8,128)S(1)} %get-tuple-element.19.direction_ref, f32[1,256,256]{2,1,0:T(8,128)S(1)} %copy-done, f32[1,256,256]{2,1,0:T(8,128)S(1)} %copy-done.1), custom_call_target="tpu_custom_call" | custom-call | flops 100000000 | tf_op jit(solution)/shard_map/pallas_call | solution.py:96
  30.8 0.5 collective-permute-start.12
  31.3 1.2 %collective-permute-start.7 = (f32[2,128]{1,0:T(2,128)S(1)}, f32[2,128]{1,0:T(2,128)S(1)}, u32[]{:S(2)}, u32[]{:S(2)}) collective-permute-start(f32[2,128]{1,0:T(2,128)S(1)} %get-tuple-element.18), channel_id=1, source_target_pairs={{0,4},{4,0},{8,12},{12,8},{16,20},{20,16},{24,28},{28,24},{1,5},{5... | collective-permute-start | bytes 3080 | tf_op jit(solution)/shard_map/ppermute | solution.py:265
  32.5 2.4 %collective-permute-done.7 = f32[2,128]{1,0:T(2,128)S(1)} collective-permute-done((f32[2,128]{1,0:T(2,128)S(1)}, f32[2,128]{1,0:T(2,128)S(1)}, u32[]{:S(2)}, u32[]{:S(2)}) %collective-permute-start.7) | collective-permute-done | bytes 1056 | tf_op jit(solution)/shard_map/ppermute | solution.py:265
  34.9 2.4 %collective-permute-start.8 = (f32[2,128]{1,0:T(2,128)S(1)}, f32[2,128]{1,0:T(2,128)S(1)}, u32[]{:S(2)}, u32[]{:S(2)}) collective-permute-start(f32[2,128]{1,0:T(2,128)S(1)} %add.55), channel_id=1, source_target_pairs={{0,8},{4,12},{8,0},{12,4},{16,24},{20,28},{24,16},{28,20},{1,9},{5... | collective-permute-start | bytes 3080 | tf_op jit(solution)/shard_map/ppermute | solution.py:265
  37.3 1.6 %collective-permute-done.8 = f32[2,128]{1,0:T(2,128)S(1)} collective-permute-done((f32[2,128]{1,0:T(2,128)S(1)}, f32[2,128]{1,0:T(2,128)S(1)}, u32[]{:S(2)}, u32[]{:S(2)}) %collective-permute-start.8) | collective-permute-done | bytes 1056 | tf_op jit(solution)/shard_map/ppermute | solution.py:265
  38.8 2.1 %collective-permute-start.9 = (f32[2,128]{1,0:T(2,128)S(1)}, f32[2,128]{1,0:T(2,128)S(1)}, u32[]{:S(2)}, u32[]{:S(2)}) collective-permute-start(f32[2,128]{1,0:T(2,128)S(1)} %add.56), channel_id=1, source_target_pairs={{0,16},{4,20},{8,24},{12,28},{16,0},{20,4},{24,8},{28,12},{1,17},{... | collective-permute-start | bytes 3080 | tf_op jit(solution)/shard_map/ppermute | solution.py:265
  40.9 2.6 %collective-permute-done.9 = f32[2,128]{1,0:T(2,128)S(1)} collective-permute-done((f32[2,128]{1,0:T(2,128)S(1)}, f32[2,128]{1,0:T(2,128)S(1)}, u32[]{:S(2)}, u32[]{:S(2)}) %collective-permute-start.9) | collective-permute-done | bytes 1056 | tf_op jit(solution)/shard_map/ppermute | solution.py:265
  43.5 0.0 collective-permute-start.10
  43.5 1.2 %collective-permute-done.10 = f32[2,128]{1,0:T(2,128)S(1)} collective-permute-done((f32[2,128]{1,0:T(2,128)S(1)}, f32[2,128]{1,0:T(2,128)S(1)}, u32[]{:S(2)}, u32[]{:S(2)}) %collective-permute-start.10) | collective-permute-done | bytes 1056 | tf_op jit(solution)/shard_map/ppermute | solution.py:265
  44.7 1.6 %collective-permute-start.11 = (f32[2,128]{1,0:T(2,128)S(1)}, f32[2,128]{1,0:T(2,128)S(1)}, u32[]{:S(2)}, u32[]{:S(2)}) collective-permute-start(f32[2,128]{1,0:T(2,128)S(1)} %add.58), channel_id=1, source_target_pairs={{0,2},{1,3},{2,0},{3,1},{4,6},{5,7},{6,4},{7,5},{8,10},{9,11},{10,... | collective-permute-start | bytes 3080 | tf_op jit(solution)/shard_map/ppermute | solution.py:265
  46.3 2.0 %collective-permute-done.11 = f32[2,128]{1,0:T(2,128)S(1)} collective-permute-done((f32[2,128]{1,0:T(2,128)S(1)}, f32[2,128]{1,0:T(2,128)S(1)}, u32[]{:S(2)}, u32[]{:S(2)}) %collective-permute-start.11) | collective-permute-done | bytes 1056 | tf_op jit(solution)/shard_map/ppermute | solution.py:265
  48.2 0.0 copy-start.4
  48.2 0.0 copy-start.5
  48.3 0.0 collective-permute-done.12.refs_1_
  48.3 0.1 shard_map.129.refs_0_
  48.3 1.5 %collective-permute-start.15 = (bf16[2,256,256]{2,1,0:T(8,128)(2,1)S(1)}, bf16[2,256,256]{2,1,0:T(8,128)(2,1)S(1)}, u32[]{:S(2)}, u32[]{:S(2)}) collective-permute-start(bf16[2,256,256]{2,1,0:T(8,128)(2,1)S(1)} %shard_map.129.refs_0_), channel_id=1, source_target_pairs={{0,12},{4,8},{8,4},{12,0},{16,28},{20,24},{24,20},{28,16},{1,13},{... | collective-permute-start | bytes 786440 | tf_op jit(solution)/shard_map/ppermute | solution.py:265
  49.8 2.7 %collective-permute-start.14 = (bf16[2,256,256]{2,1,0:T(8,128)(2,1)S(1)}, bf16[2,256,256]{2,1,0:T(8,128)(2,1)S(1)}, u32[]{:S(2)}, u32[]{:S(2)}) collective-permute-start(bf16[2,256,256]{2,1,0:T(8,128)(2,1)S(1)} %shard_map.129.refs_0_), channel_id=1, source_target_pairs={{0,8},{4,12},{8,0},{12,4},{16,24},{20,28},{24,16},{28,20},{1,9},{5... | collective-permute-start | bytes 786440 | tf_op jit(solution)/shard_map/ppermute | solution.py:265
  52.4 0.0 collective-permute-start.13
  52.4 0.0 copy-done.4
  52.4 0.0 copy-done.5
  52.4 11.8 %refresh.1 = (f32[1,256,256]{2,1,0:T(8,128)}, f32[1,256,256]{2,1,0:T(8,128)}, f32[1,256,256]{2,1,0:T(8,128)}, f32[1,256,256]{2,1,0:T(8,128)}, f32[1,256,256]{2,1,0:T(8,128)}, /*index=5*/f32[1,256,256]{2,1,0:T(8,128)}) custom-call(f32[1,256,256]{2,1,0:T(8,128)S(1)} %get-tuple-element.20.grad_ref, f32[1,256,256]{2,1,0:T(8,128)S(1)} %get-tuple-element.21.momentum_ref, ...), custom_call_target="tpu_custom_call" | custom-call | flops 2000000000 | tf_op jit(solution)/shard_map/refresh/pallas_call | solution.py:215
  64.3 0.0 collective-permute-done.15.refs_3_
  64.3 0.0 collective-permute-done.14.refs_2_
  64.3 0.0 collective-permute-done.13.refs_1_
  64.3 1.0 %assemble.1 = bf16[256,2048]{1,0:T(8,128)(2,1)} custom-call(s32[1]{0:T(128)} %bitcast.at_ref, bf16[2,256,256]{2,1,0:T(8,128)(2,1)S(1)} %shard_map.129.refs_0_, bf16[2,256,256]{2,1,0:T(8,128)(2,1)S(1)} %collective-permute-done.13.refs_1_, bf16[2,256,256]{2,1,0:T(8,128)(2,1)S(1)} %collective-permute-done.14.refs_2_, ...), custom_call_target="tpu_custom_call" | custom-call | flops 1000000 | tf_op jit(solution)/shard_map/assemble/pallas_call | solution.py:251
  (5 shorter events, 0.0 us)
Async XLA Ops:
  1.8 7.9 %collective-permute-start.5 = (bf16[1,256,256]{2,1,0:T(8,128)(2,1)S(1)}, bf16[1,256,256]{2,1,0:T(8,128)(2,1)S(1)}, u32[]{:S(2)}, u32[]{:S(2)}) collective-permute-start(bf16[1,256,256]{2,1,0:T(8,128)(2,1)S(1)} %get-tuple-element.29), channel_id=1, source_target_pairs={{0,12},{4,8},{8,4},{12,0},{16,28},{20,24},{24,20},{28,16},{1,13},{... | collective-permute-start | bytes 393224 | tf_op jit(solution)/shard_map/ppermute | solution.py:265
  5.8 6.3 %collective-permute-start.3 = (bf16[1,256,256]{2,1,0:T(8,128)(2,1)S(1)}, bf16[1,256,256]{2,1,0:T(8,128)(2,1)S(1)}, u32[]{:S(2)}, u32[]{:S(2)}) collective-permute-start(bf16[1,256,256]{2,1,0:T(8,128)(2,1)S(1)} %get-tuple-element.30), channel_id=1, source_target_pairs={{0,4},{4,0},{8,12},{12,8},{16,20},{20,16},{24,28},{28,24},{1,5},{5... | collective-permute-start | bytes 393224 | tf_op jit(solution)/shard_map/ppermute | solution.py:265
  6.3 5.9 %collective-permute-start.4 = (bf16[1,256,256]{2,1,0:T(8,128)(2,1)S(1)}, bf16[1,256,256]{2,1,0:T(8,128)(2,1)S(1)}, u32[]{:S(2)}, u32[]{:S(2)}) collective-permute-start(bf16[1,256,256]{2,1,0:T(8,128)(2,1)S(1)} %get-tuple-element.31), channel_id=1, source_target_pairs={{0,8},{4,12},{8,0},{12,4},{16,24},{20,28},{24,16},{28,20},{1,9},{5... | collective-permute-start | bytes 393224 | tf_op jit(solution)/shard_map/ppermute | solution.py:265
  6.4 21.9 %copy-start.3 = (f32[1,256,256]{2,1,0:T(8,128)S(1)}, f32[1,256,256]{2,1,0:T(8,128)}, u32[]{:S(2)}) copy-start(f32[1,256,256]{2,1,0:T(8,128)} %refs_6_.1) | copy-start | bytes 786436
  12.3 16.0 %copy-start = (f32[1,256,256]{2,1,0:T(8,128)S(1)}, f32[1,256,256]{2,1,0:T(8,128)}, u32[]{:S(2)}) copy-start(f32[1,256,256]{2,1,0:T(8,128)} %left_basis.1) | copy-start | bytes 786436
  12.3 16.0 %copy-start.1 = (f32[1,256,256]{2,1,0:T(8,128)S(1)}, f32[1,256,256]{2,1,0:T(8,128)}, u32[]{:S(2)}) copy-start(f32[1,256,256]{2,1,0:T(8,128)} %right_basis.1) | copy-start | bytes 786436
  12.3 16.1 %copy-start.2 = (f32[1,256,256]{2,1,0:T(8,128)S(1)}, f32[1,256,256]{2,1,0:T(8,128)}, u32[]{:S(2)}) copy-start(f32[1,256,256]{2,1,0:T(8,128)} %refs_5_.1) | copy-start | bytes 786436
  12.3 16.0 %collective-permute-start.6 = (f32[1,256,256]{2,1,0:T(8,128)S(1)}, f32[1,256,256]{2,1,0:T(8,128)S(1)}, u32[]{:S(2)}, u32[]{:S(2)}) collective-permute-start(f32[1,256,256]{2,1,0:T(8,128)S(1)} %shard_map.126), channel_id=1, source_target_pairs={{0,16},{4,20},{8,24},{12,28},{16,0},{20,4},{24,8},{28,12},{1,17},{... | collective-permute-start | bytes 786440 | tf_op jit(solution)/shard_map/ppermute | solution.py:265
  15.0 12.8 %collective-permute-start.2 = (bf16[1,256,256]{2,1,0:T(8,128)(2,1)S(1)}, bf16[1,256,256]{2,1,0:T(8,128)(2,1)S(1)}, u32[]{:S(2)}, u32[]{:S(2)}) collective-permute-start(bf16[1,256,256]{2,1,0:T(8,128)(2,1)S(1)} %get-tuple-element.33), channel_id=1, source_target_pairs={{0,12},{4,8},{8,4},{12,0},{16,28},{20,24},{24,20},{28,16},{1,13},{... | collective-permute-start | bytes 393224 | tf_op jit(solution)/shard_map/ppermute | solution.py:265
  16.7 11.6 %collective-permute-start.1 = (bf16[1,256,256]{2,1,0:T(8,128)(2,1)S(1)}, bf16[1,256,256]{2,1,0:T(8,128)(2,1)S(1)}, u32[]{:S(2)}, u32[]{:S(2)}) collective-permute-start(bf16[1,256,256]{2,1,0:T(8,128)(2,1)S(1)} %get-tuple-element.34), channel_id=1, source_target_pairs={{0,8},{4,12},{8,0},{12,4},{16,24},{20,28},{24,16},{28,20},{1,9},{5... | collective-permute-start | bytes 393224 | tf_op jit(solution)/shard_map/ppermute | solution.py:265
  17.9 10.4 %collective-permute-start = (bf16[1,256,256]{2,1,0:T(8,128)(2,1)S(1)}, bf16[1,256,256]{2,1,0:T(8,128)(2,1)S(1)}, u32[]{:S(2)}, u32[]{:S(2)}) collective-permute-start(bf16[1,256,256]{2,1,0:T(8,128)(2,1)S(1)} %get-tuple-element.35), channel_id=1, source_target_pairs={{0,4},{4,0},{8,12},{12,8},{16,20},{20,16},{24,28},{28,24},{1,5},{5... | collective-permute-start | bytes 393224 | tf_op jit(solution)/shard_map/ppermute | solution.py:265
  30.8 17.5 %collective-permute-start.12 = (f32[1,256,256]{2,1,0:T(8,128)S(1)}, f32[1,256,256]{2,1,0:T(8,128)S(1)}, u32[]{:S(2)}, u32[]{:S(2)}) collective-permute-start(f32[1,256,256]{2,1,0:T(8,128)S(1)} %shard_map.128.refs_0_), channel_id=1, source_target_pairs={{0,16},{4,20},{8,24},{12,28},{16,0},{20,4},{24,8},{28,12},{1,17},{... | collective-permute-start | bytes 786440 | tf_op jit(solution)/shard_map/ppermute | solution.py:265
  31.3 3.6 %collective-permute-start.7 = (f32[2,128]{1,0:T(2,128)S(1)}, f32[2,128]{1,0:T(2,128)S(1)}, u32[]{:S(2)}, u32[]{:S(2)}) collective-permute-start(f32[2,128]{1,0:T(2,128)S(1)} %get-tuple-element.18), channel_id=1, source_target_pairs={{0,4},{4,0},{8,12},{12,8},{16,20},{20,16},{24,28},{28,24},{1,5},{5... | collective-permute-start | bytes 3080 | tf_op jit(solution)/shard_map/ppermute | solution.py:265
  34.9 3.9 %collective-permute-start.8 = (f32[2,128]{1,0:T(2,128)S(1)}, f32[2,128]{1,0:T(2,128)S(1)}, u32[]{:S(2)}, u32[]{:S(2)}) collective-permute-start(f32[2,128]{1,0:T(2,128)S(1)} %add.55), channel_id=1, source_target_pairs={{0,8},{4,12},{8,0},{12,4},{16,24},{20,28},{24,16},{28,20},{1,9},{5... | collective-permute-start | bytes 3080 | tf_op jit(solution)/shard_map/ppermute | solution.py:265
  38.8 4.7 %collective-permute-start.9 = (f32[2,128]{1,0:T(2,128)S(1)}, f32[2,128]{1,0:T(2,128)S(1)}, u32[]{:S(2)}, u32[]{:S(2)}) collective-permute-start(f32[2,128]{1,0:T(2,128)S(1)} %add.56), channel_id=1, source_target_pairs={{0,16},{4,20},{8,24},{12,28},{16,0},{20,4},{24,8},{28,12},{1,17},{... | collective-permute-start | bytes 3080 | tf_op jit(solution)/shard_map/ppermute | solution.py:265
  43.5 1.2 %collective-permute-start.10 = (f32[2,128]{1,0:T(2,128)S(1)}, f32[2,128]{1,0:T(2,128)S(1)}, u32[]{:S(2)}, u32[]{:S(2)}) collective-permute-start(f32[2,128]{1,0:T(2,128)S(1)} %add.57), channel_id=1, source_target_pairs={{0,1},{1,0},{2,3},{3,2},{4,5},{5,4},{6,7},{7,6},{8,9},{9,8},{10,11... | collective-permute-start | bytes 3080 | tf_op jit(solution)/shard_map/ppermute | solution.py:265
  44.7 3.6 %collective-permute-start.11 = (f32[2,128]{1,0:T(2,128)S(1)}, f32[2,128]{1,0:T(2,128)S(1)}, u32[]{:S(2)}, u32[]{:S(2)}) collective-permute-start(f32[2,128]{1,0:T(2,128)S(1)} %add.58), channel_id=1, source_target_pairs={{0,2},{1,3},{2,0},{3,1},{4,6},{5,7},{6,4},{7,5},{8,10},{9,11},{10,... | collective-permute-start | bytes 3080 | tf_op jit(solution)/shard_map/ppermute | solution.py:265
  48.2 4.2 %copy-start.4 = (f32[1,256,256]{2,1,0:T(8,128)S(1)}, f32[1,256,256]{2,1,0:T(8,128)}, u32[]{:S(2)}) copy-start(f32[1,256,256]{2,1,0:T(8,128)} %left_stat.1) | copy-start | bytes 786436
  48.2 4.2 %copy-start.5 = (f32[1,256,256]{2,1,0:T(8,128)S(1)}, f32[1,256,256]{2,1,0:T(8,128)}, u32[]{:S(2)}) copy-start(f32[1,256,256]{2,1,0:T(8,128)} %right_stat.1) | copy-start | bytes 786436
  48.3 16.0 %collective-permute-start.15 = (bf16[2,256,256]{2,1,0:T(8,128)(2,1)S(1)}, bf16[2,256,256]{2,1,0:T(8,128)(2,1)S(1)}, u32[]{:S(2)}, u32[]{:S(2)}) collective-permute-start(bf16[2,256,256]{2,1,0:T(8,128)(2,1)S(1)} %shard_map.129.refs_0_), channel_id=1, source_target_pairs={{0,12},{4,8},{8,4},{12,0},{16,28},{20,24},{24,20},{28,16},{1,13},{... | collective-permute-start | bytes 786440 | tf_op jit(solution)/shard_map/ppermute | solution.py:265
  49.8 14.5 %collective-permute-start.14 = (bf16[2,256,256]{2,1,0:T(8,128)(2,1)S(1)}, bf16[2,256,256]{2,1,0:T(8,128)(2,1)S(1)}, u32[]{:S(2)}, u32[]{:S(2)}) collective-permute-start(bf16[2,256,256]{2,1,0:T(8,128)(2,1)S(1)} %shard_map.129.refs_0_), channel_id=1, source_target_pairs={{0,8},{4,12},{8,0},{12,4},{16,24},{20,28},{24,16},{28,20},{1,9},{5... | collective-permute-start | bytes 786440 | tf_op jit(solution)/shard_map/ppermute | solution.py:265
  52.4 11.9 %collective-permute-start.13 = (bf16[2,256,256]{2,1,0:T(8,128)(2,1)S(1)}, bf16[2,256,256]{2,1,0:T(8,128)(2,1)S(1)}, u32[]{:S(2)}, u32[]{:S(2)}) collective-permute-start(bf16[2,256,256]{2,1,0:T(8,128)(2,1)S(1)} %shard_map.129.refs_0_), channel_id=1, source_target_pairs={{0,4},{4,0},{8,12},{12,8},{16,20},{20,16},{24,28},{28,24},{1,5},{5... | collective-permute-start | bytes 786440 | tf_op jit(solution)/shard_map/ppermute | solution.py:265

commit v3 on v2

--- a/solution.py
+++ b/solution.py
@@ -1,3 +1,6 @@
+import functools
+import math
+
 import jax
 import jax.numpy as jnp
 from jax import lax
@@ -13,6 +16,8 @@
 SUB = 8
 LANES = 128
 PANEL = 32
+PARTS = 1
+HEAD_PANELS = 3
 KERNEL_BYTES = 16 * 2**20
 
 
@@ -42,10 +47,11 @@
     return jnp.broadcast_to(value[at:at + 1, :], (SUB, LANES))
 
 
-def eliminate(work, order, rows):
+def eliminate(work, rows, begin, end):
+    order = work.shape[0]
     tiles = 2 * order // LANES
     groups = PANEL // SUB
-    for start in range(0, order, PANEL):
+    for start in range(begin, end, PANEL):
         first = start // LANES
         live = range(first, tiles)
         held = [
@@ -91,7 +97,7 @@
     return pltpu.with_memory_space_constraint(value, pltpu.VMEM)
 
 
-def local_call(body, outs, args, flops, scratch=()):
+def local_call(body, outs, args, flops, scratch=(), aliases=None):
     whole = pl.BlockSpec(memory_space=pltpu.VMEM)
     return pl.pallas_call(
         body,
@@ -99,6 +105,7 @@
         in_specs=[whole] * len(args),
         out_specs=(whole,) * len(outs),
         scratch_shapes=list(scratch),
+        input_output_aliases=aliases or {},
         cost_estimate=pl.CostEstimate(flops=flops, transcendentals=0, bytes_accessed=0),
         compiler_params=pltpu.CompilerParams(vmem_limit_bytes=KERNEL_BYTES),
     )(*[in_vmem(value) for value in args])
@@ -122,14 +129,16 @@
     return jnp.sum(value * value, axis=0, keepdims=True)
 
 
-def rotate(pieces, momentum, second, left_basis, right_basis):
-    count = len(pieces)
+def rotate(pieces, across, momentum, second, left_basis, right_basis):
+    split_at = len(pieces)
+    count = split_at + len(across)
 
     def body(*refs):
         momentum_ref, second_ref, left_ref, right_ref = refs[count:count + 4]
         grad_out, momentum_out, second_out, direction_out, norm_out = refs[count + 4:]
         order = left_ref.shape[1]
-        gradient = total(refs[:count])
+        far_sum = jnp.concatenate([ref[0] for ref in refs[split_at:count]], axis=0)
+        gradient = total(refs[:split_at]) + far_sum
         grad_out[0] = gradient
         moment = beta_first * momentum_ref[0] + (1.0 - beta_first) * gradient
         momentum_out[0] = moment
@@ -147,7 +156,7 @@
     whole = (momentum.shape, jnp.float32)
     return local_call(
         body, [whole] * 4 + [((2, LANES), jnp.float32)],
-        [*pieces, momentum, second, left_basis, right_basis], 3 * 10**8,
+        [*pieces, *across, momentum, second, left_basis, right_basis], 3 * 10**8,
     )
 
 
@@ -174,11 +183,44 @@
     return local_call(body, [(shape, jnp.bfloat16)], [norms, *steps], 10**6)[0]
 
 
-def refresh_body(grad_ref, momentum_ref, second_ref, left_stat, left_basis, right_stat, right_basis,
+def prepare(gradient, left_stat, left_basis, right_stat, right_basis):
+    def body(grad_ref, left_stat_ref, left_ref, right_stat_ref, right_ref,
+             left_new, right_new, left_work, right_work):
+        order = left_ref.shape[1]
+        gradient = grad_ref[0]
+        left_new[0] = beta_second * left_stat_ref[0] + (1.0 - beta_second) * dot(gradient, gradient, 1, 1)
+        right_new[0] = beta_second * right_stat_ref[0] + (1.0 - beta_second) * dot(gradient, gradient, 0, 0)
+        for stat, basis, work in ((left_new, left_ref, left_work), (right_new, right_ref, right_work)):
+            powered_t = dot(basis[0], stat[0], 0, 0)
+            work[:, order:] = powered_t
+            work[:, :order] = dot(powered_t, powered_t, 1, 1)
+
+    shape = left_stat.shape
+    work = ((shape[-1], 2 * shape[-1]), jnp.float32)
+    return local_call(
+        body, [(shape, jnp.float32)] * 2 + [work] * 2,
+        [gradient, left_stat, left_basis, right_stat, right_basis], 5 * 10**8,
+    )
+
+
+def eliminate_both(left_work, right_work, begin, end):
+    rows = lax.broadcasted_iota(jnp.int32, (SUB, LANES), 0)
+    for _ in zip(eliminate(left_work, rows, begin, end), eliminate(right_work, rows, begin, end)):
+        pass
+
+
+def begin_refresh(left_work, right_work, end):
+    def body(left_in, right_in, left_out, right_out):
+        eliminate_both(left_out, right_out, 0, end)
+
+    work = (left_work.shape, jnp.float32)
+    return local_call(body, [work] * 2, [left_work, right_work], 6 * 10**8, aliases={0: 0, 1: 1})
+
+
+def refresh_body(begin, momentum_ref, second_ref, left_new, right_new, left_in, right_in,
                  momentum_out, second_out, left_out, right_out, left_basis_out, right_basis_out,
-                 left_new, right_new, left_turned, right_turned, left_work, right_work, sems):
-    order = left_stat.shape[1]
-    rows = lax.broadcasted_iota(jnp.int32, (SUB, LANES), 0)
+                 left_work, right_work, left_turned, right_turned, sems):
+    order = left_new.shape[1]
     copies = []
 
     def write(source, target):
@@ -187,17 +229,9 @@
 
     write(momentum_ref, momentum_out)
     write(second_ref, second_out)
-    gradient = grad_ref[0]
-    left_new[0] = beta_second * left_stat[0] + (1.0 - beta_second) * dot(gradient, gradient, 1, 1)
     write(left_new, left_out)
-    right_new[0] = beta_second * right_stat[0] + (1.0 - beta_second) * dot(gradient, gradient, 0, 0)
     write(right_new, right_out)
-    for stat, basis, work in ((left_new, left_basis, left_work), (right_new, right_basis, right_work)):
-        powered_t = dot(basis[0], stat[0], 0, 0)
-        work[:, order:] = powered_t
-        work[:, :order] = dot(powered_t, powered_t, 1, 1)
-    for _ in zip(eliminate(left_work, order, rows), eliminate(right_work, order, rows)):
-        pass
+    eliminate_both(left_work, right_work, begin, order)
     left_turned[0] = left_work[:, order:].T
     write(left_turned, left_basis_out)
     right_turned[0] = right_work[:, order:].T
@@ -206,22 +240,23 @@
         copy.wait()
 
 
-def refresh(gradient, momentum_new, second_new, left_stat, left_basis, right_stat, right_basis):
-    shape = left_stat.shape
-    order = shape[-1]
-    args = [gradient, momentum_new, second_new, left_stat, left_basis, right_stat, right_basis]
+def refresh(momentum_new, second_new, left_new, right_new, left_work, right_work, begin):
+    shape = left_new.shape
+    args = [momentum_new, second_new, left_new, right_new, left_work, right_work]
     block = pltpu.VMEM(shape, jnp.float32)
-    work = pltpu.VMEM((order, 2 * order), jnp.float32)
+    whole = pl.BlockSpec(memory_space=pltpu.VMEM)
     return pl.pallas_call(
-        refresh_body,
-        out_shape=(jax.ShapeDtypeStruct(shape, jnp.float32),) * 6,
-        in_specs=[pl.BlockSpec(memory_space=pltpu.VMEM)] * len(args),
-        out_specs=(pl.BlockSpec(memory_space=pl.ANY),) * 6,
-        scratch_shapes=[block] * 4 + [work] * 2 + [pltpu.SemaphoreType.DMA((6,))],
+        functools.partial(refresh_body, begin),
+        out_shape=(jax.ShapeDtypeStruct(shape, jnp.float32),) * 6
+        + (pltpu.VMEM(left_work.shape, jnp.float32),) * 2,
+        in_specs=[whole] * len(args),
+        out_specs=(pl.BlockSpec(memory_space=pl.ANY),) * 6 + (whole,) * 2,
+        input_output_aliases={4: 6, 5: 7},
+        scratch_shapes=[block] * 2 + [pltpu.SemaphoreType.DMA((6,))],
         cost_estimate=pl.CostEstimate(flops=2 * 10**9, transcendentals=0, bytes_accessed=0),
         compiler_params=pltpu.CompilerParams(vmem_limit_bytes=KERNEL_BYTES),
         name="refresh",
-    )(*[in_vmem(value) for value in args])
+    )(*[in_vmem(value) for value in args])[:6]
 
 
 def assemble(at, gathered, far, row_count, shard_width):
@@ -260,17 +295,22 @@
     )(jnp.reshape(at, (1,)), *[in_vmem(value) for _, value in gathered])
 
 
-def swap(value, axis, size, step):
+def swap(value, axes, size, step):
     pairs = [(at, at ^ step) for at in range(size)]
-    return lax.ppermute(value, axis, pairs)
+    return lax.ppermute(value, axes, pairs)
 
 
 def all_sum(value, sizes):
-    for axis in sizes:
-        step = 1
-        while step < sizes[axis]:
-            value = value + swap(value, axis, sizes[axis], step)
-            step *= 2
+    axes = tuple(sizes)
+    count = math.prod(sizes.values())
+    low = 1
+    while low < count:
+        paired = low > 1 and 4 * low <= count
+        others = [swap(value, axes, count, times * low) for times in range(1, 4 if paired else 2)]
+        value = value + others[0]
+        if paired:
+            value = value + (others[1] + others[2])
+        low *= 4 if paired else 2
     return value
 
 
@@ -288,18 +328,23 @@
         row_band = lax.div(number, jnp.int32(col_bands))
         return row_band * order, (number - row_band * col_bands) * order
 
-    def chunk(step):
-        return lax.dynamic_slice(source, corner(at ^ step), (order, order))[None]
-
-    source = replica_part
-
-    first = [swap(chunk(far ^ step), "dp", replicas, step) for step in near]
+    def chunk(source, step, part=0, parts=1):
+        top, edge = corner(at ^ step)
+        rows = order // parts
+        return lax.dynamic_slice(source, (top + part * rows, edge), (rows, order))[None]
+
+    first = [
+        [swap(chunk(replica_part, far ^ step, part, PARTS), "dp", replicas, step) for step in near]
+        for part in range(PARTS)
+    ]
     source = lax.optimization_barrier(replica_part)
-    half = add_pieces([chunk(far)] + first)
-    across = swap(half, "dp", replicas, far)
-    second_hop = [swap(chunk(step), "dp", replicas, step) for step in near]
+    across = [
+        swap(add_pieces([chunk(source, far, part, PARTS)] + first[part]), "dp", replicas, far)
+        for part in range(PARTS)
+    ]
+    second_hop = [swap(chunk(source, step), "dp", replicas, step) for step in near]
     gradient, momentum_new, second_new, direction, norm_local = rotate(
-        [chunk(0)] + second_hop + [across], momentum, second, left_basis, right_basis
+        [chunk(source, 0)] + second_hop, across, momentum, second, left_basis, right_basis
     )
     norms = all_sum(norm_local, sizes)
     raw_step = rotate_back(direction, left_basis, right_basis)
@@ -307,8 +352,13 @@
     pair = scale_steps(norms, [raw_step, raw_across])
     gathered = [(0, pair)] + [(step, swap(pair, "dp", replicas, step)) for step in near]
     assembled = assemble(at, gathered, far, row_count, shard_width)
+    left_new, right_new, left_work, right_work = prepare(
+        gradient, left_stat, left_basis, right_stat, right_basis
+    )
+    begin = min(HEAD_PANELS * PANEL, order)
+    left_work, right_work = begin_refresh(left_work, right_work, begin)
     momentum_new, second_new, left_new, right_new, left_basis_new, right_basis_new = refresh(
-        gradient, momentum_new, second_new, left_stat, left_basis, right_stat, right_basis
+        momentum_new, second_new, left_new, right_new, left_work, right_work, begin
     )
     return (
         assembled,

time: 65.5 us -> 66.2 us (1.011)
    pallas_call x4 -> x6, Pallas kernels: 2.54 us -> 8.31 us  [local_call(): pl.pallas_call(body, out_shape=tuple((pltpu.VMEM(shape, dtype) for shape,...]
    pallas_call x1, Pallas kernels: 11.8 us -> 6.27 us  [refresh(): pl.pallas_call(functools.partial(refresh_body, begin), out_shape=(jax.Sha...]
    ppermute x16 -> x18, waiting for transfers between devices: 24 us -> 24.6 us  [swap(): return lax.ppermute(value, axes, pairs)]
    ppermute x16 -> x18, starting transfers between devices: 22.8 us -> 22.7 us  [swap(): return lax.ppermute(value, axes, pairs)]
  transfers between devices with their start and end apart: 16 -> 18, of which waited for: 10 -> 10; matrix products, arithmetic and copies ran while one was open for 2% -> 2% of each run, Pallas kernels for 18% -> 20%
where the time goes in v3:
time: 66.2 us; the launch traced here: 66 us
  waiting for transfers between devices  24.6 us (37%)
  starting transfers between devices  22.7 us (34%)
  Pallas kernels  15.6 us (24%)
  local copies, waits for them, and re-layouts  2.35 us (4%)
  between operations  0.82 us (1%)
    ppermute x18, waiting for transfers between devices, swap(): return lax.ppermute(value, axes, pairs)  24.6 us
    ppermute x18, starting transfers between devices, swap(): return lax.ppermute(value, axes, pairs)  22.7 us
    pallas_call x6, Pallas kernels, local_call(): pl.pallas_call(body, out_shape=tuple((pltpu.VMEM(shape, dtype) for shape,...  8.31 us
    pallas_call x1, Pallas kernels, refresh(): pl.pallas_call(functools.partial(refresh_body, begin), out_shape=(jax.Sha...  6.27 us
  transfers between devices with their start and end apart: 18, of which 10 were waited for; matrix products, arithmetic and copies ran while one was open for 2% of the time, Pallas kernels for 20%

profile of v3, /device:TPU:0, one launch (start us, length us, event | category | flops | bytes accessed | tf_op | source)
XLA Modules:
  0.0 66.0 jit_solution(7685903728584849251)
XLA Ops:
  0.7 1.1 %constant_dynamic-slice_fusion = (bf16[1,256,256]{2,1,0:T(8,128)(2,1)S(1)}, bf16[1,256,256]{2,1,0:T(8,128)(2,1)S(1)}, bf16[1,256,256]{2,1,0:T(8,128)(2,1)S(1)}) fusion(bf16[1,256,2048]{2,1,0:T(8,128)(2,1)} %param.7, s32[]{:T(128)S(6)} %select_n.39, s32[]{:T(128)S(6)} %select_n.37, s32[]{:T(128)S(6)} %select_n.38), kind=kLoop, calls=%fused_computation.5 | loop fusion | bytes 786444 | tf_op jit(solution)/shard_map/dynamic_slice | solution.py:334
  1.8 3.0 %collective-permute-start.3 = (bf16[1,256,256]{2,1,0:T(8,128)(2,1)S(1)}, bf16[1,256,256]{2,1,0:T(8,128)(2,1)S(1)}, u32[]{:S(2)}, u32[]{:S(2)}) collective-permute-start(bf16[1,256,256]{2,1,0:T(8,128)(2,1)S(1)} %get-tuple-element.42), channel_id=1, source_target_pairs={{0,4},{4,0},{8,12},{12,8},{16,20},{20,16},{24,28},{28,24},{1,5},{5... | collective-permute-start | bytes 393224 | tf_op jit(solution)/shard_map/ppermute | solution.py:300
  4.8 1.6 %collective-permute-start.4 = (bf16[1,256,256]{2,1,0:T(8,128)(2,1)S(1)}, bf16[1,256,256]{2,1,0:T(8,128)(2,1)S(1)}, u32[]{:S(2)}, u32[]{:S(2)}) collective-permute-start(bf16[1,256,256]{2,1,0:T(8,128)(2,1)S(1)} %get-tuple-element.43), channel_id=1, source_target_pairs={{0,8},{4,12},{8,0},{12,4},{16,24},{20,28},{24,16},{28,20},{1,9},{5... | collective-permute-start | bytes 393224 | tf_op jit(solution)/shard_map/ppermute | solution.py:300
  6.4 0.0 collective-permute-start.5
  6.4 0.0 copy-start.3
  6.4 1.3 %dynamic-slice_bitcast_fusion = (bf16[1,256,256]{2,1,0:T(8,128)(2,1)S(1)}, bf16[1,256,256]{2,1,0:T(8,128)(2,1)S(1)}, bf16[1,256,256]{2,1,0:T(8,128)(2,1)S(1)}, b...) fusion(bf16[256,2048]{1,0:T(8,128)(2,1)} %bitcast.12, s32[]{:T(128)S(6)} %select_n.36, s32[]{:T(128)S(6)} %select_n.35, ...), kind=kLoop, calls=%fused_computation | loop fusion | bytes 1310740 | tf_op jit(solution)/shard_map/broadcast_in_dim | solution.py:334
  7.6 0.7 collective-permute-done.3.refs_1_
  8.3 2.9 %collective-permute-done.4.refs_2_ = bf16[1,256,256]{2,1,0:T(8,128)(2,1)S(1)} collective-permute-done((bf16[1,256,256]{2,1,0:T(8,128)(2,1)S(1)}, bf16[1,256,256]{2,1,0:T(8,128)(2,1)S(1)}, u32[]{:S(2)}, u32[]{:S(2)}) %collective-permute-start.4) | collective-permute-done | bytes 131104 | tf_op jit(solution)/shard_map/ppermute | solution.py:300
  11.1 1.2 %collective-permute-done.5.refs_3_ = bf16[1,256,256]{2,1,0:T(8,128)(2,1)S(1)} collective-permute-done((bf16[1,256,256]{2,1,0:T(8,128)(2,1)S(1)}, bf16[1,256,256]{2,1,0:T(8,128)(2,1)S(1)}, u32[]{:S(2)}, u32[]{:S(2)}) %collective-permute-start.5) | collective-permute-done | bytes 131104 | tf_op jit(solution)/shard_map/ppermute | solution.py:300
  12.4 0.0 copy-start
  12.4 0.0 copy-start.1
  12.4 0.0 copy-start.2
  12.4 0.1 shard_map.126
  12.4 2.8 %collective-permute-start.6 = (f32[1,256,256]{2,1,0:T(8,128)S(1)}, f32[1,256,256]{2,1,0:T(8,128)S(1)}, u32[]{:S(2)}, u32[]{:S(2)}) collective-permute-start(f32[1,256,256]{2,1,0:T(8,128)S(1)} %shard_map.126), channel_id=1, source_target_pairs={{0,16},{4,20},{8,24},{12,28},{16,0},{20,4},{24,8},{28,12},{1,17},{... | collective-permute-start | bytes 786440 | tf_op jit(solution)/shard_map/ppermute | solution.py:300
  15.3 1.5 %collective-permute-start = (bf16[1,256,256]{2,1,0:T(8,128)(2,1)S(1)}, bf16[1,256,256]{2,1,0:T(8,128)(2,1)S(1)}, u32[]{:S(2)}, u32[]{:S(2)}) collective-permute-start(bf16[1,256,256]{2,1,0:T(8,128)(2,1)S(1)} %get-tuple-element.47), channel_id=1, source_target_pairs={{0,4},{4,0},{8,12},{12,8},{16,20},{20,16},{24,28},{28,24},{1,5},{5... | collective-permute-start | bytes 393224 | tf_op jit(solution)/shard_map/ppermute | solution.py:300
  16.7 1.6 %collective-permute-start.1 = (bf16[1,256,256]{2,1,0:T(8,128)(2,1)S(1)}, bf16[1,256,256]{2,1,0:T(8,128)(2,1)S(1)}, u32[]{:S(2)}, u32[]{:S(2)}) collective-permute-start(bf16[1,256,256]{2,1,0:T(8,128)(2,1)S(1)} %get-tuple-element.46), channel_id=1, source_target_pairs={{0,8},{4,12},{8,0},{12,4},{16,24},{20,28},{24,16},{28,20},{1,9},{5... | collective-permute-start | bytes 393224 | tf_op jit(solution)/shard_map/ppermute | solution.py:300
  18.3 0.4 collective-permute-start.2
  18.8 2.3 %collective-permute-done.refs_1_ = bf16[1,256,256]{2,1,0:T(8,128)(2,1)S(1)} collective-permute-done((bf16[1,256,256]{2,1,0:T(8,128)(2,1)S(1)}, bf16[1,256,256]{2,1,0:T(8,128)(2,1)S(1)}, u32[]{:S(2)}, u32[]{:S(2)}) %collective-permute-start) | collective-permute-done | bytes 131104 | tf_op jit(solution)/shard_map/ppermute | solution.py:300
  21.1 5.4 %collective-permute-done.1.refs_2_ = bf16[1,256,256]{2,1,0:T(8,128)(2,1)S(1)} collective-permute-done((bf16[1,256,256]{2,1,0:T(8,128)(2,1)S(1)}, bf16[1,256,256]{2,1,0:T(8,128)(2,1)S(1)}, u32[]{:S(2)}, u32[]{:S(2)}) %collective-permute-start.1) | collective-permute-done | bytes 131104 | tf_op jit(solution)/shard_map/ppermute | solution.py:300
  26.5 1.6 %collective-permute-done.2.refs_3_ = bf16[1,256,256]{2,1,0:T(8,128)(2,1)S(1)} collective-permute-done((bf16[1,256,256]{2,1,0:T(8,128)(2,1)S(1)}, bf16[1,256,256]{2,1,0:T(8,128)(2,1)S(1)}, u32[]{:S(2)}, u32[]{:S(2)}) %collective-permute-start.2) | collective-permute-done | bytes 131104 | tf_op jit(solution)/shard_map/ppermute | solution.py:300
  28.1 0.0 collective-permute-done.6.refs_4_
  28.1 0.0 copy-done.3
  28.1 0.0 copy-done
  28.1 0.0 copy-done.1
  28.1 0.0 copy-done.2
  28.1 1.4 %shard_map.127 = (f32[1,256,256]{2,1,0:T(8,128)S(1)}, f32[1,256,256]{2,1,0:T(8,128)S(1)}, f32[1,256,256]{2,1,0:T(8,128)S(1)}, f32[1,256,256]{2,1,0:T(8,128)S(1)}, f32[2,128]{1,0:T(2,128)S(1)}) custom-call(bf16[1,256,256]{2,1,0:T(8,128)(2,1)S(1)} %get-tuple-element.48.refs_0_, bf16[1,256,256]{2,1,0:T(8,128)(2,1)S(1)} %collective-permute-done.refs_1_, ...), custom_call_target="tpu_custom_call" | custom-call | flops 300000000 | tf_op jit(solution)/shard_map/pallas_call | solution.py:102
  29.5 0.0 collective-permute-start.7
  29.5 1.2 %collective-permute-done.7 = f32[2,128]{1,0:T(2,128)S(1)} collective-permute-done((f32[2,128]{1,0:T(2,128)S(1)}, f32[2,128]{1,0:T(2,128)S(1)}, u32[]{:S(2)}, u32[]{:S(2)}) %collective-permute-start.7) | collective-permute-done | bytes 1056 | tf_op jit(solution)/shard_map/ppermute | solution.py:300
  30.7 2.2 %collective-permute-start.10 = (f32[2,128]{1,0:T(2,128)S(1)}, f32[2,128]{1,0:T(2,128)S(1)}, u32[]{:S(2)}, u32[]{:S(2)}) collective-permute-start(f32[2,128]{1,0:T(2,128)S(1)} %add.61), channel_id=1, source_target_pairs={{0,6},{1,7},{2,4},{3,5},{4,2},{5,3},{6,0},{7,1},{8,14},{9,15},{10,... | collective-permute-start | bytes 3080 | tf_op jit(solution)/shard_map/ppermute | solution.py:300
  32.9 0.5 collective-permute-start.8
  33.4 0.8 %collective-permute-start.9 = (f32[2,128]{1,0:T(2,128)S(1)}, f32[2,128]{1,0:T(2,128)S(1)}, u32[]{:S(2)}, u32[]{:S(2)}) collective-permute-start(f32[2,128]{1,0:T(2,128)S(1)} %add.61), channel_id=1, source_target_pairs={{0,4},{1,5},{2,6},{3,7},{4,0},{5,1},{6,2},{7,3},{8,12},{9,13},{10,... | collective-permute-start | bytes 3080 | tf_op jit(solution)/shard_map/ppermute | solution.py:300
  34.2 1.0 %shard_map.128.refs_0_ = f32[1,256,256]{2,1,0:T(8,128)S(1)} custom-call(f32[1,256,256]{2,1,0:T(8,128)S(1)} %get-tuple-element.25.direction_ref, f32[1,256,256]{2,1,0:T(8,128)S(1)} %copy-done, f32[1,256,256]{2,1,0:T(8,128)S(1)} %copy-done.1), custom_call_target="tpu_custom_call" | custom-call | flops 100000000 | tf_op jit(solution)/shard_map/pallas_call | solution.py:102
  35.2 0.3 collective-permute-start.14
  35.5 0.0 collective-permute-done.10
  35.5 1.0 %collective-permute-done.8 = f32[2,128]{1,0:T(2,128)S(1)} collective-permute-done((f32[2,128]{1,0:T(2,128)S(1)}, f32[2,128]{1,0:T(2,128)S(1)}, u32[]{:S(2)}, u32[]{:S(2)}) %collective-permute-start.8) | collective-permute-done | bytes 1056 | tf_op jit(solution)/shard_map/ppermute | solution.py:300
  36.5 0.5 collective-permute-done.9
  37.0 0.3 collective-permute-start.11
  37.3 1.7 %collective-permute-start.12 = (f32[2,128]{1,0:T(2,128)S(1)}, f32[2,128]{1,0:T(2,128)S(1)}, u32[]{:S(2)}, u32[]{:S(2)}) collective-permute-start(f32[2,128]{1,0:T(2,128)S(1)} %add_add_fusion.1), channel_id=1, source_target_pairs={{0,16},{1,17},{2,18},{3,19},{4,20},{5,21},{6,22},{7,23},{8,24},{9,... | collective-permute-start | bytes 3080 | tf_op jit(solution)/shard_map/ppermute | solution.py:300
  39.0 2.4 %collective-permute-start.13 = (f32[2,128]{1,0:T(2,128)S(1)}, f32[2,128]{1,0:T(2,128)S(1)}, u32[]{:S(2)}, u32[]{:S(2)}) collective-permute-start(f32[2,128]{1,0:T(2,128)S(1)} %add_add_fusion.1), channel_id=1, source_target_pairs={{0,24},{1,25},{2,26},{3,27},{4,28},{5,29},{6,30},{7,31},{8,16},{9,... | collective-permute-start | bytes 3080 | tf_op jit(solution)/shard_map/ppermute | solution.py:300
  41.4 0.0 collective-permute-done.11
  41.4 7.9 %collective-permute-done.12 = f32[2,128]{1,0:T(2,128)S(1)} collective-permute-done((f32[2,128]{1,0:T(2,128)S(1)}, f32[2,128]{1,0:T(2,128)S(1)}, u32[]{:S(2)}, u32[]{:S(2)}) %collective-permute-start.12) | collective-permute-done | bytes 1056 | tf_op jit(solution)/shard_map/ppermute | solution.py:300
  49.2 0.0 collective-permute-done.13
  49.2 0.0 copy-start.4
  49.3 0.0 copy-start.5
  49.3 0.0 collective-permute-done.14.refs_1_
  49.3 0.1 shard_map.129.refs_0_
  49.3 1.2 %collective-permute-start.15 = (bf16[2,256,256]{2,1,0:T(8,128)(2,1)S(1)}, bf16[2,256,256]{2,1,0:T(8,128)(2,1)S(1)}, u32[]{:S(2)}, u32[]{:S(2)}) collective-permute-start(bf16[2,256,256]{2,1,0:T(8,128)(2,1)S(1)} %shard_map.129.refs_0_), channel_id=1, source_target_pairs={{0,4},{4,0},{8,12},{12,8},{16,20},{20,16},{24,28},{28,24},{1,5},{5... | collective-permute-start | bytes 786440 | tf_op jit(solution)/shard_map/ppermute | solution.py:300
  50.6 0.5 collective-permute-start.16
  51.1 1.8 %collective-permute-start.17 = (bf16[2,256,256]{2,1,0:T(8,128)(2,1)S(1)}, bf16[2,256,256]{2,1,0:T(8,128)(2,1)S(1)}, u32[]{:S(2)}, u32[]{:S(2)}) collective-permute-start(bf16[2,256,256]{2,1,0:T(8,128)(2,1)S(1)} %shard_map.129.refs_0_), channel_id=1, source_target_pairs={{0,12},{4,8},{8,4},{12,0},{16,28},{20,24},{24,20},{28,16},{1,13},{... | collective-permute-start | bytes 786440 | tf_op jit(solution)/shard_map/ppermute | solution.py:300
  52.9 0.0 copy-done.4
  52.9 0.0 copy-done.5
  52.9 2.1 %shard_map.130 = (f32[1,256,256]{2,1,0:T(8,128)S(1)}, f32[1,256,256]{2,1,0:T(8,128)S(1)}, f32[256,512]{1,0:T(8,128)S(1)}, f32[256,512]{1,0:T(8,128)S(1)}) custom-call(f32[1,256,256]{2,1,0:T(8,128)S(1)} %get-tuple-element.28.grad_ref, f32[1,256,256]{2,1,0:T(8,128)S(1)} %copy-done.4, f32[1,256,256]{2,1,0:T(8,128)S(1)} %copy-done, ...), custom_call_target="tpu_custom_call" | custom-call | flops 500000000 | tf_op jit(solution)/shard_map/pallas_call | solution.py:102
  55.0 3.7 %shard_map.131 = (f32[256,512]{1,0:T(8,128)S(1)}, f32[256,512]{1,0:T(8,128)S(1)}) custom-call(f32[256,512]{1,0:T(8,128)S(1)} %get-tuple-element.31.left_in, f32[256,512]{1,0:T(8,128)S(1)} %get-tuple-element.32.right_in), custom_call_target="tpu_custom_call", output_to_operand_aliasing={{0}: (0, {}), {1}: (1, {})} | custom-call | flops 600000000 | tf_op jit(solution)/shard_map/pallas_call | solution.py:102
  58.7 6.3 %refresh.1 = (f32[1,256,256]{2,1,0:T(8,128)}, f32[1,256,256]{2,1,0:T(8,128)}, f32[1,256,256]{2,1,0:T(8,128)}, f32[1,256,256]{2,1,0:T(8,128)}, f32[1,256,256]{2,1...) custom-call(f32[1,256,256]{2,1,0:T(8,128)S(1)} %get-tuple-element.26, ...), custom_call_target="tpu_custom_call", output_to_operand_aliasing={{6}: (4, {}), {7}: (5, {})} | custom-call | flops 2000000000 | tf_op jit(solution)/shard_map/refresh/pallas_call | solution.py:248
  65.0 0.0 collective-permute-done.15.refs_1_
  65.0 0.0 collective-permute-done.16.refs_2_
  65.0 0.0 collective-permute-done.17.refs_3_
  65.0 1.0 %assemble.1 = bf16[256,2048]{1,0:T(8,128)(2,1)} custom-call(s32[1]{0:T(128)} %bitcast.at_ref, bf16[2,256,256]{2,1,0:T(8,128)(2,1)S(1)} %shard_map.129.refs_0_, bf16[2,256,256]{2,1,0:T(8,128)(2,1)S(1)} %collective-permute-done.15.refs_1_, bf16[2,256,256]{2,1,0:T(8,128)(2,1)S(1)} %collective-permute-done.16.refs_2_, ...), custom_call_target="tpu_custom_call" | custom-call | flops 1000000 | tf_op jit(solution)/shard_map/assemble/pallas_call | solution.py:286
  (3 shorter events, 0.0 us)
Async XLA Ops:
  1.8 6.5 %collective-permute-start.3 = (bf16[1,256,256]{2,1,0:T(8,128)(2,1)S(1)}, bf16[1,256,256]{2,1,0:T(8,128)(2,1)S(1)}, u32[]{:S(2)}, u32[]{:S(2)}) collective-permute-start(bf16[1,256,256]{2,1,0:T(8,128)(2,1)S(1)} %get-tuple-element.42), channel_id=1, source_target_pairs={{0,4},{4,0},{8,12},{12,8},{16,20},{20,16},{24,28},{28,24},{1,5},{5... | collective-permute-start | bytes 393224 | tf_op jit(solution)/shard_map/ppermute | solution.py:300
  4.8 6.4 %collective-permute-start.4 = (bf16[1,256,256]{2,1,0:T(8,128)(2,1)S(1)}, bf16[1,256,256]{2,1,0:T(8,128)(2,1)S(1)}, u32[]{:S(2)}, u32[]{:S(2)}) collective-permute-start(bf16[1,256,256]{2,1,0:T(8,128)(2,1)S(1)} %get-tuple-element.43), channel_id=1, source_target_pairs={{0,8},{4,12},{8,0},{12,4},{16,24},{20,28},{24,16},{28,20},{1,9},{5... | collective-permute-start | bytes 393224 | tf_op jit(solution)/shard_map/ppermute | solution.py:300
  6.4 6.0 %collective-permute-start.5 = (bf16[1,256,256]{2,1,0:T(8,128)(2,1)S(1)}, bf16[1,256,256]{2,1,0:T(8,128)(2,1)S(1)}, u32[]{:S(2)}, u32[]{:S(2)}) collective-permute-start(bf16[1,256,256]{2,1,0:T(8,128)(2,1)S(1)} %get-tuple-element.41), channel_id=1, source_target_pairs={{0,12},{4,8},{8,4},{12,0},{16,28},{20,24},{24,20},{28,16},{1,13},{... | collective-permute-start | bytes 393224 | tf_op jit(solution)/shard_map/ppermute | solution.py:300
  6.4 21.7 %copy-start.3 = (f32[1,256,256]{2,1,0:T(8,128)S(1)}, f32[1,256,256]{2,1,0:T(8,128)}, u32[]{:S(2)}) copy-start(f32[1,256,256]{2,1,0:T(8,128)} %refs_6_.1) | copy-start | bytes 786436
  12.4 15.7 %copy-start = (f32[1,256,256]{2,1,0:T(8,128)S(1)}, f32[1,256,256]{2,1,0:T(8,128)}, u32[]{:S(2)}) copy-start(f32[1,256,256]{2,1,0:T(8,128)} %left_ref.3) | copy-start | bytes 786436
  12.4 15.7 %copy-start.1 = (f32[1,256,256]{2,1,0:T(8,128)S(1)}, f32[1,256,256]{2,1,0:T(8,128)}, u32[]{:S(2)}) copy-start(f32[1,256,256]{2,1,0:T(8,128)} %right_ref.3) | copy-start | bytes 786436
  12.4 15.8 %copy-start.2 = (f32[1,256,256]{2,1,0:T(8,128)S(1)}, f32[1,256,256]{2,1,0:T(8,128)}, u32[]{:S(2)}) copy-start(f32[1,256,256]{2,1,0:T(8,128)} %refs_5_.1) | copy-start | bytes 786436
  12.4 15.7 %collective-permute-start.6 = (f32[1,256,256]{2,1,0:T(8,128)S(1)}, f32[1,256,256]{2,1,0:T(8,128)S(1)}, u32[]{:S(2)}, u32[]{:S(2)}) collective-permute-start(f32[1,256,256]{2,1,0:T(8,128)S(1)} %shard_map.126), channel_id=1, source_target_pairs={{0,16},{4,20},{8,24},{12,28},{16,0},{20,4},{24,8},{28,12},{1,17},{... | collective-permute-start | bytes 786440 | tf_op jit(solution)/shard_map/ppermute | solution.py:300
  15.3 5.8 %collective-permute-start = (bf16[1,256,256]{2,1,0:T(8,128)(2,1)S(1)}, bf16[1,256,256]{2,1,0:T(8,128)(2,1)S(1)}, u32[]{:S(2)}, u32[]{:S(2)}) collective-permute-start(bf16[1,256,256]{2,1,0:T(8,128)(2,1)S(1)} %get-tuple-element.47), channel_id=1, source_target_pairs={{0,4},{4,0},{8,12},{12,8},{16,20},{20,16},{24,28},{28,24},{1,5},{5... | collective-permute-start | bytes 393224 | tf_op jit(solution)/shard_map/ppermute | solution.py:300
  16.7 9.7 %collective-permute-start.1 = (bf16[1,256,256]{2,1,0:T(8,128)(2,1)S(1)}, bf16[1,256,256]{2,1,0:T(8,128)(2,1)S(1)}, u32[]{:S(2)}, u32[]{:S(2)}) collective-permute-start(bf16[1,256,256]{2,1,0:T(8,128)(2,1)S(1)} %get-tuple-element.46), channel_id=1, source_target_pairs={{0,8},{4,12},{8,0},{12,4},{16,24},{20,28},{24,16},{28,20},{1,9},{5... | collective-permute-start | bytes 393224 | tf_op jit(solution)/shard_map/ppermute | solution.py:300
  18.3 9.8 %collective-permute-start.2 = (bf16[1,256,256]{2,1,0:T(8,128)(2,1)S(1)}, bf16[1,256,256]{2,1,0:T(8,128)(2,1)S(1)}, u32[]{:S(2)}, u32[]{:S(2)}) collective-permute-start(bf16[1,256,256]{2,1,0:T(8,128)(2,1)S(1)} %get-tuple-element.45), channel_id=1, source_target_pairs={{0,12},{4,8},{8,4},{12,0},{16,28},{20,24},{24,20},{28,16},{1,13},{... | collective-permute-start | bytes 393224 | tf_op jit(solution)/shard_map/ppermute | solution.py:300
  29.5 1.2 %collective-permute-start.7 = (f32[2,128]{1,0:T(2,128)S(1)}, f32[2,128]{1,0:T(2,128)S(1)}, u32[]{:S(2)}, u32[]{:S(2)}) collective-permute-start(f32[2,128]{1,0:T(2,128)S(1)} %get-tuple-element.24), channel_id=1, source_target_pairs={{0,1},{1,0},{2,3},{3,2},{4,5},{5,4},{6,7},{7,6},{8,9},{9,8},{10,11... | collective-permute-start | bytes 3080 | tf_op jit(solution)/shard_map/ppermute | solution.py:300
  30.7 4.8 %collective-permute-start.10 = (f32[2,128]{1,0:T(2,128)S(1)}, f32[2,128]{1,0:T(2,128)S(1)}, u32[]{:S(2)}, u32[]{:S(2)}) collective-permute-start(f32[2,128]{1,0:T(2,128)S(1)} %add.61), channel_id=1, source_target_pairs={{0,6},{1,7},{2,4},{3,5},{4,2},{5,3},{6,0},{7,1},{8,14},{9,15},{10,... | collective-permute-start | bytes 3080 | tf_op jit(solution)/shard_map/ppermute | solution.py:300
  32.9 3.6 %collective-permute-start.8 = (f32[2,128]{1,0:T(2,128)S(1)}, f32[2,128]{1,0:T(2,128)S(1)}, u32[]{:S(2)}, u32[]{:S(2)}) collective-permute-start(f32[2,128]{1,0:T(2,128)S(1)} %add.61), channel_id=1, source_target_pairs={{0,2},{1,3},{2,0},{3,1},{4,6},{5,7},{6,4},{7,5},{8,10},{9,11},{10,... | collective-permute-start | bytes 3080 | tf_op jit(solution)/shard_map/ppermute | solution.py:300
  33.4 3.6 %collective-permute-start.9 = (f32[2,128]{1,0:T(2,128)S(1)}, f32[2,128]{1,0:T(2,128)S(1)}, u32[]{:S(2)}, u32[]{:S(2)}) collective-permute-start(f32[2,128]{1,0:T(2,128)S(1)} %add.61), channel_id=1, source_target_pairs={{0,4},{1,5},{2,6},{3,7},{4,0},{5,1},{6,2},{7,3},{8,12},{9,13},{10,... | collective-permute-start | bytes 3080 | tf_op jit(solution)/shard_map/ppermute | solution.py:300
  35.2 14.1 %collective-permute-start.14 = (f32[1,256,256]{2,1,0:T(8,128)S(1)}, f32[1,256,256]{2,1,0:T(8,128)S(1)}, u32[]{:S(2)}, u32[]{:S(2)}) collective-permute-start(f32[1,256,256]{2,1,0:T(8,128)S(1)} %shard_map.128.refs_0_), channel_id=1, source_target_pairs={{0,16},{4,20},{8,24},{12,28},{16,0},{20,4},{24,8},{28,12},{1,17},{... | collective-permute-start | bytes 786440 | tf_op jit(solution)/shard_map/ppermute | solution.py:300
  37.0 4.4 %collective-permute-start.11 = (f32[2,128]{1,0:T(2,128)S(1)}, f32[2,128]{1,0:T(2,128)S(1)}, u32[]{:S(2)}, u32[]{:S(2)}) collective-permute-start(f32[2,128]{1,0:T(2,128)S(1)} %add_add_fusion.1), channel_id=1, source_target_pairs={{0,8},{1,9},{2,10},{3,11},{4,12},{5,13},{6,14},{7,15},{8,0},{9,1},... | collective-permute-start | bytes 3080 | tf_op jit(solution)/shard_map/ppermute | solution.py:300
  37.3 11.9 %collective-permute-start.12 = (f32[2,128]{1,0:T(2,128)S(1)}, f32[2,128]{1,0:T(2,128)S(1)}, u32[]{:S(2)}, u32[]{:S(2)}) collective-permute-start(f32[2,128]{1,0:T(2,128)S(1)} %add_add_fusion.1), channel_id=1, source_target_pairs={{0,16},{1,17},{2,18},{3,19},{4,20},{5,21},{6,22},{7,23},{8,24},{9,... | collective-permute-start | bytes 3080 | tf_op jit(solution)/shard_map/ppermute | solution.py:300
  39.0 10.3 %collective-permute-start.13 = (f32[2,128]{1,0:T(2,128)S(1)}, f32[2,128]{1,0:T(2,128)S(1)}, u32[]{:S(2)}, u32[]{:S(2)}) collective-permute-start(f32[2,128]{1,0:T(2,128)S(1)} %add_add_fusion.1), channel_id=1, source_target_pairs={{0,24},{1,25},{2,26},{3,27},{4,28},{5,29},{6,30},{7,31},{8,16},{9,... | collective-permute-start | bytes 3080 | tf_op jit(solution)/shard_map/ppermute | solution.py:300
  49.2 3.7 %copy-start.4 = (f32[1,256,256]{2,1,0:T(8,128)S(1)}, f32[1,256,256]{2,1,0:T(8,128)}, u32[]{:S(2)}) copy-start(f32[1,256,256]{2,1,0:T(8,128)} %left_stat_ref.1) | copy-start | bytes 786436
  49.3 3.6 %copy-start.5 = (f32[1,256,256]{2,1,0:T(8,128)S(1)}, f32[1,256,256]{2,1,0:T(8,128)}, u32[]{:S(2)}) copy-start(f32[1,256,256]{2,1,0:T(8,128)} %right_stat_ref.1) | copy-start | bytes 786436
  49.3 15.6 %collective-permute-start.15 = (bf16[2,256,256]{2,1,0:T(8,128)(2,1)S(1)}, bf16[2,256,256]{2,1,0:T(8,128)(2,1)S(1)}, u32[]{:S(2)}, u32[]{:S(2)}) collective-permute-start(bf16[2,256,256]{2,1,0:T(8,128)(2,1)S(1)} %shard_map.129.refs_0_), channel_id=1, source_target_pairs={{0,4},{4,0},{8,12},{12,8},{16,20},{20,16},{24,28},{28,24},{1,5},{5... | collective-permute-start | bytes 786440 | tf_op jit(solution)/shard_map/ppermute | solution.py:300
  50.6 14.4 %collective-permute-start.16 = (bf16[2,256,256]{2,1,0:T(8,128)(2,1)S(1)}, bf16[2,256,256]{2,1,0:T(8,128)(2,1)S(1)}, u32[]{:S(2)}, u32[]{:S(2)}) collective-permute-start(bf16[2,256,256]{2,1,0:T(8,128)(2,1)S(1)} %shard_map.129.refs_0_), channel_id=1, source_target_pairs={{0,8},{4,12},{8,0},{12,4},{16,24},{20,28},{24,16},{28,20},{1,9},{5... | collective-permute-start | bytes 786440 | tf_op jit(solution)/shard_map/ppermute | solution.py:300
  51.1 13.9 %collective-permute-start.17 = (bf16[2,256,256]{2,1,0:T(8,128)(2,1)S(1)}, bf16[2,256,256]{2,1,0:T(8,128)(2,1)S(1)}, u32[]{:S(2)}, u32[]{:S(2)}) collective-permute-start(bf16[2,256,256]{2,1,0:T(8,128)(2,1)S(1)} %shard_map.129.refs_0_), channel_id=1, source_target_pairs={{0,12},{4,8},{8,4},{12,0},{16,28},{20,24},{24,20},{28,16},{1,13},{... | collective-permute-start | bytes 786440 | tf_op jit(solution)/shard_map/ppermute | solution.py:300
